TPU v7x, 256 devices: a whole 4x4x8 slice. The times are simulated.
256 devices in a mesh: member: 8 (over y, x_lo), space: 32 (over z, x_hi, core).
Axes of the slice: x: 4 (x_hi: 2, x_lo: 2; x = x_hi * 2 + x_lo), y: 4, z: 8, core: 2. Of those that a mesh axis runs over, the one named last changes fastest.
Arguments:
- hidden_codes: bfloat16 [16, 256, 92160], P('member', None, 'space'), may hold values from -6 to 6
- w_in: bfloat16 [1024, 256], replicated, may hold values from -0.375 to 0.375
- b_in: float32 [1024], replicated, may hold values from -3 to 3
- w_out: bfloat16 [72, 1024], replicated, may hold values from -0.1875 to 0.1875
- b_out: float32 [72], replicated, may hold values from -3 to 3
- target: bfloat16 [72, 92160], P(None, 'space'), may hold values from -6 to 6
- band_start: int32 [32], P('space'), may hold values from 0 to 62, as said below
Outputs:
- code_sensitivity: bfloat16 [16, 256, 92160], P('member', None, 'space')
- grad_w_in: float32 [1024, 256], replicated
- grad_w_out: float32 [72, 1024], replicated
- grad_b_in: float32 [1024], replicated
Inputs may be any that keep to these rules, and one draw needn't show every extreme that they name: band_start holds each of 0, 2, 4, ... once, in some order.
All inputs are finite; a program needn't handle non-finite values.
Results may differ from a plain program's by a relative error of at most 0.005.
The roundings to bfloat16 on the way count: a program that leaves them out, or rounds other values in their place, can miss the bound.
Values may be sent and summed in bfloat16 or wider, within the bound.
No kernel may reach another device: no remote copies, remote signals or barrier semaphores. Data moves between devices by JAX's collectives and lax.ppermute only.
A program may use at most 128 MiB of HBM per device.

v0:
```python
import math

import jax
import jax.numpy as jnp
from jax import lax
from jax.sharding import PartitionSpec as P

LON = 1440


def split_up(array, dim, devices):
    dims = array.shape
    parts = array.reshape(*dims[:dim], devices, dims[dim] // devices, *dims[dim + 1 :])
    return jnp.moveaxis(parts, dim, 0)


def edges_of(length, count):
    unit = 8 if length >= 8 * count else 1
    return [length // unit * k // count * unit for k in range(1, count)]


def joined_along(parts, dim):
    dims = list(parts.shape[1:])
    dims[dim] *= parts.shape[0]
    return jnp.moveaxis(parts, 0, dim).reshape(dims)


def exchange_in_pieces(array, axis, pieces, split_dim, concat_dim):
    parts = split_up(array, split_dim, lax.axis_size(axis))
    cut = max(range(1, max(2, parts.ndim - 1)), key=lambda d: parts.shape[d])
    gathered = []
    for piece in jnp.split(parts, edges_of(parts.shape[cut], pieces), axis=cut):
        if piece.size:
            gathered.append(lax.all_to_all(piece, axis, split_axis=0, concat_axis=0, tiled=True))
    return joined_along(jnp.concatenate(gathered, axis=cut), concat_dim)


def sent_and_summed(array, axis, dim):
    devices = lax.axis_size(axis)
    parts = lax.all_to_all(split_up(array, dim, devices), axis, 0, 0, tiled=True)
    return jnp.sum(parts.astype(jnp.float32), axis=0)


def copy_for_each(array, axis):
    devices = lax.axis_size(axis)
    return lax.all_to_all(
        jnp.broadcast_to(array[None], (devices, *array.shape)), axis, 0, 0, tiled=True
    )


def of_everyone(array, axis):
    everything = copy_for_each(array, axis)
    return jnp.sum(everything, axis=0)


def gathered_copies(array, axis, dim):
    parts = copy_for_each(array, axis)
    return joined_along(parts, dim)


def slope(diff):
    return diff / jnp.sqrt(diff * diff + 0.0625)


def pairwise_total(values, tiles):

    def lone_realization(total, other):
        return (total + slope(values - other.astype(jnp.float32)[None]), None)

    total, discarded_value = lax.scan(lone_realization, jnp.zeros_like(values), tiles)
    return total


def on_device(hidden_codes, w_in, b_in, w_out, b_out, target, band_start):
    local_members = hidden_codes.shape[0]
    cells = hidden_codes.shape[2]
    rows = cells // LON
    lat_rows = rows * lax.axis_size("space")
    members = local_members * lax.axis_size("member")
    angle = ((band_start[0] + jnp.arange(rows, dtype=jnp.int32)).astype(jnp.float32) + 0.5) * (
        math.pi / lat_rows
    ) - math.pi / 2
    area = jnp.broadcast_to(jnp.cos(angle)[:, None], (rows, LON)).reshape(cells)
    saved = []
    mapped_predictions = []
    for ensemble_position in range(local_members):
        pre = (
            jnp.dot(w_in, hidden_codes[ensemble_position], preferred_element_type=jnp.float32)
            + b_in[:, None]
        )
        act_f, undo = jax.vjp(jax.nn.gelu, pre)
        act = act_f.astype(jnp.bfloat16)
        saved.append((act, undo))
        mapped_predictions.append(
            (jnp.dot(w_out, act, preferred_element_type=jnp.float32) + b_out[:, None]).astype(
                jnp.bfloat16
            )
        )
    predicted_maps = jnp.stack(mapped_predictions)
    diagonal_contribution = predicted_maps.astype(jnp.float32)
    block = lax.all_to_all(predicted_maps, "member", split_axis=2, concat_axis=0, tiled=True)
    total = pairwise_total(block.astype(jnp.float32), block)
    couple_index = exchange_in_pieces(total, "member", 2, 0, 2)
    goal = target.astype(jnp.float32)[None]
    prediction_sensitivity = (
        area[None, None, :] * (slope(diagonal_contribution - goal) - couple_index / members)
    ).astype(jnp.bfloat16)
    adjoint_entry_matrix = jnp.zeros(w_in.shape, jnp.float32)
    adjoint_exit_matrix = jnp.zeros(w_out.shape, jnp.float32)
    g_bias = jnp.zeros(b_in.shape, jnp.float32)
    grads = []
    for ensemble_position in range(local_members):
        act, undo = saved[ensemble_position]
        prediction_adjoint = prediction_sensitivity[ensemble_position]
        dact = jnp.dot(w_out.T, prediction_adjoint, preferred_element_type=jnp.float32)
        dpre = undo(dact)[0].astype(jnp.bfloat16)
        grads.append(jnp.dot(w_in.T, dpre, preferred_element_type=jnp.float32).astype(jnp.bfloat16))
        adjoint_entry_matrix = adjoint_entry_matrix + jnp.dot(
            dpre, hidden_codes[ensemble_position].T, preferred_element_type=jnp.float32
        )
        adjoint_exit_matrix = adjoint_exit_matrix + jnp.dot(
            prediction_adjoint, act.T, preferred_element_type=jnp.float32
        )
        g_bias = g_bias + jnp.sum(dpre.astype(jnp.float32), axis=1)
    code_sensitivity = jnp.stack(grads)
    stacked = jnp.concatenate(
        [adjoint_entry_matrix, adjoint_exit_matrix.T, g_bias[:, None]], axis=1
    )
    shares = sent_and_summed(stacked.astype(jnp.bfloat16), "space", 0)
    shares = of_everyone(shares, "member")
    summed = gathered_copies(shares, "space", 0)
    scale = 1.0 / math.sqrt(members * cells)
    latent_width = w_in.shape[1]
    channel_count = w_out.shape[0]
    grad_w_in = summed[:, :latent_width] * scale
    grad_w_out = summed[:, latent_width : latent_width + channel_count].T * scale
    grad_b_in = summed[:, latent_width + channel_count] * scale
    return (code_sensitivity, grad_w_in, grad_w_out, grad_b_in)


def solution(mesh):
    in_specs = (P("member", None, "space"), P(), P(), P(), P(), P(None, "space"), P("space"))
    out_specs = (P("member", None, "space"), P(), P(), P())
    return jax.shard_map(
        on_device, mesh=mesh, in_specs=in_specs, out_specs=out_specs, check_vma=False
    )
```

profile of v0, /device:TPU:1, one launch (start us, length us, event | category | flops | bytes accessed | tf_op | source)
XLA Modules:
  0.0 273.2 jit_solution(17318421373382060209)
XLA Ops:
  0.7 1.0 copy-done
  1.7 7.5 %fusion.29 = f32[1024,2880]{0,1:T(8,128)} fusion(bf16[1024,256]{1,0:T(8,128)(2,1)S(1)} %copy-done, bf16[2,256,2880]{1,2,0:T(8,128)(2,1)} %param.9), kind=kOutput, calls=%fused_computation.51 | convolution fusion | flops 1509949440 | bytes 13795328 | tf_op jit(solution)/shard_map/dot_general | solution.py:88
  9.2 12.6 %multiply_convert_fusion.1 = (bf16[1024,2880]{0,1:T(8,128)(2,1)S(1)}, bf16[1024,2880]{0,1:T(8,128)(2,1)S(1)}, f32[1024,2880]{0,1:T(8,128)}) fusion(f32[1024]{0:T(1024)S(1)} %copy-done.11, f32[1024,2880]{0,1:T(8,128)} %fusion.29, bf16[1024,256]{1,0:T(8,128)(2,1)S(1)} %copy-done, bf16[2,256,2880]{1,2,0:T(8,128)(2,1)S(1)} %copy-done.7), kind=kOutput, calls=%fused_computation.33 | convolution fusion | flops 1568931840 | bytes 37392384 | tf_op jit(solution)/shard_map/dot_general | solution.py:88
  21.8 1.9 fusion.24
  23.7 1.9 fusion.25
  25.7 0.3 copy-done.2
  26.0 0.2 copy-done.3
  26.2 0.8 copy-done.5
  27.0 0.1 pad_maximum_fusion.1
  27.1 2.9 %copy.34 = bf16[2,72,2880]{1,0,2:T(2,128)(2,1)} copy(bf16[2,72,2880]{2,1,0:T(8,128)(2,1)S(1)} %pad_maximum_fusion.1) | data formatting | bytes 1658880 | tf_op jit(solution)/shard_map/stack | solution.py:99
  30.0 5.9 %all-to-all-start = ((bf16[2,72,2880]{1,0,2:T(2,128)(2,1)}), bf16[2,72,2880]{1,0,2:T(2,128)(2,1)S(1)}, u32[]{:S(2)}, u32[]{:S(2)}) async-start(bf16[2,72,2880]{1,0,2:T(2,128)(2,1)} %copy.34), calls=%async_computation | async-start | bytes 2949120 | tf_op jit(solution)/shard_map/all_to_all | solution.py:101
  35.9 19.4 %all-to-all-done = bf16[2,72,2880]{1,0,2:T(2,128)(2,1)S(1)} async-done(((bf16[2,72,2880]{1,0,2:T(2,128)(2,1)}), bf16[2,72,2880]{1,0,2:T(2,128)(2,1)S(1)}, u32[]{:S(2)}, u32[]{:S(2)}) %all-to-all-start) | async-done | bytes 829472 | tf_op jit(solution)/shard_map/all_to_all | solution.py:101
  55.4 1.3 copy.35
  56.7 0.2 bitcast_convert_fusion.1
  56.9 48.4 %while.11 = (s32[]{:T(128)}, f32[16,72,360]{2,1,0:T(8,128)}, bf16[16,72,360]{2,1,0:T(8,128)(2,1)S(1)}, f32[16,72,360]{2,1,0:T(8,128)S(1)}, s32[]{:T(128)}, /*index=5*/s32[]{:T(128)}) while((s32[]{:T(128)}, f32[16,72,360]{2,1,0:T(8,128)}, bf16[16,72,360]{2,1,0:T(8,128)(2,1)S(1)}, f32[16,72,360]{2,1,0:T(8,128)S(1)}, s32[]{:T(128)}, ...), condition=%wide.region_1.2_spmd.clone, body=%wide.region_0.1_spmd.clone.sunk | while | flops 2514243 | bytes 5235923 | solution.py:70
  56.9 1.6 select_add_fusion.2
  58.6 3.1 %select_add_fusion.2 = f32[16,72,360]{2,1,0:T(8,128)} fusion(f32[16,72,360]{2,1,0:T(8,128)} %get-tuple-element.109, f32[16,72,360]{2,1,0:T(8,128)S(1)} %get-tuple-element.117, f32[72,360]{1,0:T(8,128)S(1)} %bitcast_convert_fusion.3, pred[]{:T(512)S(6)} %compare.3), kind=kLoop, calls=%fused_computation.clone.1 | loop fusion | flops 2488320 | bytes 5080321 | tf_op jit(solution)/shard_map/while/body/eval_jaxpr/add | solution.py:68
  61.7 3.1 %select_add_fusion.2 = f32[16,72,360]{2,1,0:T(8,128)} fusion(f32[16,72,360]{2,1,0:T(8,128)} %get-tuple-element.109, f32[16,72,360]{2,1,0:T(8,128)S(1)} %get-tuple-element.117, f32[72,360]{1,0:T(8,128)S(1)} %bitcast_convert_fusion.3, pred[]{:T(512)S(6)} %compare.3), kind=kLoop, calls=%fused_computation.clone.1 | loop fusion | flops 2488320 | bytes 5080321 | tf_op jit(solution)/shard_map/while/body/eval_jaxpr/add | solution.py:68
  64.8 3.1 %select_add_fusion.2 = f32[16,72,360]{2,1,0:T(8,128)} fusion(f32[16,72,360]{2,1,0:T(8,128)} %get-tuple-element.109, f32[16,72,360]{2,1,0:T(8,128)S(1)} %get-tuple-element.117, f32[72,360]{1,0:T(8,128)S(1)} %bitcast_convert_fusion.3, pred[]{:T(512)S(6)} %compare.3), kind=kLoop, calls=%fused_computation.clone.1 | loop fusion | flops 2488320 | bytes 5080321 | tf_op jit(solution)/shard_map/while/body/eval_jaxpr/add | solution.py:68
  67.9 3.1 %select_add_fusion.2 = f32[16,72,360]{2,1,0:T(8,128)} fusion(f32[16,72,360]{2,1,0:T(8,128)} %get-tuple-element.109, f32[16,72,360]{2,1,0:T(8,128)S(1)} %get-tuple-element.117, f32[72,360]{1,0:T(8,128)S(1)} %bitcast_convert_fusion.3, pred[]{:T(512)S(6)} %compare.3), kind=kLoop, calls=%fused_computation.clone.1 | loop fusion | flops 2488320 | bytes 5080321 | tf_op jit(solution)/shard_map/while/body/eval_jaxpr/add | solution.py:68
  71.0 3.1 %select_add_fusion.2 = f32[16,72,360]{2,1,0:T(8,128)} fusion(f32[16,72,360]{2,1,0:T(8,128)} %get-tuple-element.109, f32[16,72,360]{2,1,0:T(8,128)S(1)} %get-tuple-element.117, f32[72,360]{1,0:T(8,128)S(1)} %bitcast_convert_fusion.3, pred[]{:T(512)S(6)} %compare.3), kind=kLoop, calls=%fused_computation.clone.1 | loop fusion | flops 2488320 | bytes 5080321 | tf_op jit(solution)/shard_map/while/body/eval_jaxpr/add | solution.py:68
  74.1 3.1 %select_add_fusion.2 = f32[16,72,360]{2,1,0:T(8,128)} fusion(f32[16,72,360]{2,1,0:T(8,128)} %get-tuple-element.109, f32[16,72,360]{2,1,0:T(8,128)S(1)} %get-tuple-element.117, f32[72,360]{1,0:T(8,128)S(1)} %bitcast_convert_fusion.3, pred[]{:T(512)S(6)} %compare.3), kind=kLoop, calls=%fused_computation.clone.1 | loop fusion | flops 2488320 | bytes 5080321 | tf_op jit(solution)/shard_map/while/body/eval_jaxpr/add | solution.py:68
  77.3 3.1 %select_add_fusion.2 = f32[16,72,360]{2,1,0:T(8,128)} fusion(f32[16,72,360]{2,1,0:T(8,128)} %get-tuple-element.109, f32[16,72,360]{2,1,0:T(8,128)S(1)} %get-tuple-element.117, f32[72,360]{1,0:T(8,128)S(1)} %bitcast_convert_fusion.3, pred[]{:T(512)S(6)} %compare.3), kind=kLoop, calls=%fused_computation.clone.1 | loop fusion | flops 2488320 | bytes 5080321 | tf_op jit(solution)/shard_map/while/body/eval_jaxpr/add | solution.py:68
  80.4 3.1 %select_add_fusion.2 = f32[16,72,360]{2,1,0:T(8,128)} fusion(f32[16,72,360]{2,1,0:T(8,128)} %get-tuple-element.109, f32[16,72,360]{2,1,0:T(8,128)S(1)} %get-tuple-element.117, f32[72,360]{1,0:T(8,128)S(1)} %bitcast_convert_fusion.3, pred[]{:T(512)S(6)} %compare.3), kind=kLoop, calls=%fused_computation.clone.1 | loop fusion | flops 2488320 | bytes 5080321 | tf_op jit(solution)/shard_map/while/body/eval_jaxpr/add | solution.py:68
  83.5 3.1 %select_add_fusion.2 = f32[16,72,360]{2,1,0:T(8,128)} fusion(f32[16,72,360]{2,1,0:T(8,128)} %get-tuple-element.109, f32[16,72,360]{2,1,0:T(8,128)S(1)} %get-tuple-element.117, f32[72,360]{1,0:T(8,128)S(1)} %bitcast_convert_fusion.3, pred[]{:T(512)S(6)} %compare.3), kind=kLoop, calls=%fused_computation.clone.1 | loop fusion | flops 2488320 | bytes 5080321 | tf_op jit(solution)/shard_map/while/body/eval_jaxpr/add | solution.py:68
  86.6 3.1 %select_add_fusion.2 = f32[16,72,360]{2,1,0:T(8,128)} fusion(f32[16,72,360]{2,1,0:T(8,128)} %get-tuple-element.109, f32[16,72,360]{2,1,0:T(8,128)S(1)} %get-tuple-element.117, f32[72,360]{1,0:T(8,128)S(1)} %bitcast_convert_fusion.3, pred[]{:T(512)S(6)} %compare.3), kind=kLoop, calls=%fused_computation.clone.1 | loop fusion | flops 2488320 | bytes 5080321 | tf_op jit(solution)/shard_map/while/body/eval_jaxpr/add | solution.py:68
  89.7 3.1 %select_add_fusion.2 = f32[16,72,360]{2,1,0:T(8,128)} fusion(f32[16,72,360]{2,1,0:T(8,128)} %get-tuple-element.109, f32[16,72,360]{2,1,0:T(8,128)S(1)} %get-tuple-element.117, f32[72,360]{1,0:T(8,128)S(1)} %bitcast_convert_fusion.3, pred[]{:T(512)S(6)} %compare.3), kind=kLoop, calls=%fused_computation.clone.1 | loop fusion | flops 2488320 | bytes 5080321 | tf_op jit(solution)/shard_map/while/body/eval_jaxpr/add | solution.py:68
  92.8 3.1 %select_add_fusion.2 = f32[16,72,360]{2,1,0:T(8,128)} fusion(f32[16,72,360]{2,1,0:T(8,128)} %get-tuple-element.109, f32[16,72,360]{2,1,0:T(8,128)S(1)} %get-tuple-element.117, f32[72,360]{1,0:T(8,128)S(1)} %bitcast_convert_fusion.3, pred[]{:T(512)S(6)} %compare.3), kind=kLoop, calls=%fused_computation.clone.1 | loop fusion | flops 2488320 | bytes 5080321 | tf_op jit(solution)/shard_map/while/body/eval_jaxpr/add | solution.py:68
  96.0 3.1 %select_add_fusion.2 = f32[16,72,360]{2,1,0:T(8,128)} fusion(f32[16,72,360]{2,1,0:T(8,128)} %get-tuple-element.109, f32[16,72,360]{2,1,0:T(8,128)S(1)} %get-tuple-element.117, f32[72,360]{1,0:T(8,128)S(1)} %bitcast_convert_fusion.3, pred[]{:T(512)S(6)} %compare.3), kind=kLoop, calls=%fused_computation.clone.1 | loop fusion | flops 2488320 | bytes 5080321 | tf_op jit(solution)/shard_map/while/body/eval_jaxpr/add | solution.py:68
  99.1 3.1 %select_add_fusion.2 = f32[16,72,360]{2,1,0:T(8,128)} fusion(f32[16,72,360]{2,1,0:T(8,128)} %get-tuple-element.109, f32[16,72,360]{2,1,0:T(8,128)S(1)} %get-tuple-element.117, f32[72,360]{1,0:T(8,128)S(1)} %bitcast_convert_fusion.3, pred[]{:T(512)S(6)} %compare.3), kind=kLoop, calls=%fused_computation.clone.1 | loop fusion | flops 2488320 | bytes 5080321 | tf_op jit(solution)/shard_map/while/body/eval_jaxpr/add | solution.py:68
  102.2 3.1 %select_add_fusion.2 = f32[16,72,360]{2,1,0:T(8,128)} fusion(f32[16,72,360]{2,1,0:T(8,128)} %get-tuple-element.109, f32[16,72,360]{2,1,0:T(8,128)S(1)} %get-tuple-element.117, f32[72,360]{1,0:T(8,128)S(1)} %bitcast_convert_fusion.3, pred[]{:T(512)S(6)} %compare.3), kind=kLoop, calls=%fused_computation.clone.1 | loop fusion | flops 2488320 | bytes 5080321 | tf_op jit(solution)/shard_map/while/body/eval_jaxpr/add | solution.py:68
  105.3 2.1 split.8
  107.4 3.7 %all-to-all-start.1 = ((f32[8,2,32,360]{3,2,1,0:T(8,128)}), f32[8,2,32,360]{3,2,1,0:T(8,128)S(1)}, u32[]{:S(2)}, u32[]{:S(2)}) async-start(f32[8,2,32,360]{3,2,1,0:T(8,128)} %split.8), calls=%async_computation.1 | async-start | bytes 1572864 | tf_op jit(solution)/shard_map/all_to_all | solution.py:34
  111.1 2.2 split.9
  113.3 9.3 %all-to-all-done.1 = f32[8,2,32,360]{3,2,1,0:T(8,128)S(1)} async-done(((f32[8,2,32,360]{3,2,1,0:T(8,128)}), f32[8,2,32,360]{3,2,1,0:T(8,128)S(1)}, u32[]{:S(2)}, u32[]{:S(2)}) %all-to-all-start.1) | async-done | bytes 737312 | tf_op jit(solution)/shard_map/all_to_all | solution.py:34
  122.6 3.7 %all-to-all-start.2 = ((f32[8,2,40,360]{3,2,1,0:T(8,128)}), f32[8,2,40,360]{3,2,1,0:T(8,128)S(1)}, u32[]{:S(2)}, u32[]{:S(2)}) async-start(f32[8,2,40,360]{3,2,1,0:T(8,128)} %split.9), calls=%async_computation.2 | async-start | bytes 1966080 | tf_op jit(solution)/shard_map/all_to_all | solution.py:34
  126.3 2.0 convert_element_type.76
  129.2 0.1 mul.128
  129.2 9.6 %all-to-all-done.2 = f32[8,2,40,360]{3,2,1,0:T(8,128)S(1)} async-done(((f32[8,2,40,360]{3,2,1,0:T(8,128)}), f32[8,2,40,360]{3,2,1,0:T(8,128)S(1)}, u32[]{:S(2)}, u32[]{:S(2)}) %all-to-all-start.2) | async-done | bytes 921632 | tf_op jit(solution)/shard_map/all_to_all | solution.py:34
  138.8 0.1 fusion.26
  139.0 0.6 copy.36
  139.6 1.7 div.17
  141.3 2.3 multiply_convert_fusion.2
  143.6 11.9 %convert_reduce_fusion = (f32[1024]{0:T(1024)S(1)}, bf16[1024,2880]{0,1:T(8,128)(2,1)S(1)}) fusion(f32[1024,2880]{0,1:T(8,128)} %fusion.29, f32[1024]{0:T(1024)S(1)} %copy-done.11, bf16[72,1024]{1,0:T(8,128)(2,1)S(1)} %copy-done.9, bf16[2,72,2880]{2,1,0:T(8,128)(2,1)S(1)} %multiply_convert_fusion.2), kind=kOutput, calls=%fused_computation.30 | convolution fusion | flops 492502016 | bytes 18274304 | tf_op jit(solution)/shard_map/dot_general | solution.py:115
  155.6 1.2 fusion.48
  156.8 10.4 %convert_reduce_fusion.1 = (f32[1024]{0:T(1024)S(1)}, bf16[1024,2880]{0,1:T(8,128)(2,1)}) fusion(f32[1024,2880]{0,1:T(8,128)S(1)} %bitcast.122, f32[1024]{0:T(1024)S(1)} %copy-done.11, bf16[72,1024]{1,0:T(8,128)(2,1)S(1)} %copy-done.9, bf16[2,72,2880]{2,1,0:T(8,128)(2,1)S(1)} %multiply_convert_fusion.2), kind=kOutput, calls=%fused_computation.31 | convolution fusion | flops 492502016 | bytes 18274304 | tf_op jit(solution)/shard_map/dot_general | solution.py:115
  167.2 1.8 fusion.27
  169.1 1.2 fusion.45
  170.3 0.2 copy.37
  170.5 0.4 add.127
  170.9 4.9 %fusion.38 = bf16[1024,256]{1,0:T(8,128)(2,1)S(1)} fusion(f32[1024,256]{1,0:T(8,128)S(1)} %fusion.27, bf16[1024,2880]{0,1:T(8,128)(2,1)} %get-tuple-element.74, bf16[2,256,2880]{1,2,0:T(8,128)(2,1)} %param.9), kind=kOutput, calls=%fused_computation.58 | convolution fusion | flops 1510473728 | bytes 8945664 | tf_op jit(solution)/shard_map/dot_general | solution.py:118
  175.9 0.2 pad_maximum_fusion.2
  176.0 36.3 %all_to_all.43 = bf16[32,32,329]{2,1,0:T(8,128)(2,1)S(1)} all-to-all(bf16[32,32,329]{2,1,0:T(8,128)(2,1)S(1)} %pad_maximum_fusion.2), channel_id=1, replica_groups=mesh['member'=8,'space'=32] {'space'}, dimensions={0} | all-to-all | bytes 1347584 | tf_op jit(solution)/shard_map/all_to_all | solution.py:40
  212.4 0.1 convert_reduce_fusion.2
  212.6 10.0 %all_to_all.44 = f32[8,32,329]{2,1,0:T(8,128)S(1)} all-to-all(f32[8,32,329]{2,1,0:T(8,128)S(1)} %broadcast_in_dim.11), channel_id=1, replica_groups=mesh['member'=8,'space'=32] {'member'}, dimensions={0} | all-to-all | bytes 673792 | tf_op jit(solution)/shard_map/all_to_all | solution.py:46
  222.6 1.3 broadcast_in_dim.12
  223.9 7.1 %all-to-all-start.5 = ((f32[32,32,329]{2,1,0:T(8,128)}), f32[32,32,329]{2,1,0:T(8,128)S(1)}, u32[]{:S(2)}, u32[]{:S(2)}) async-start(f32[32,32,329]{2,1,0:T(8,128)} %broadcast_in_dim.12), calls=%async_computation.5 | async-start | bytes 3145728 | tf_op jit(solution)/shard_map/all_to_all | solution.py:46
  231.1 4.4 %fusion.20 = bf16[1,256,2880]{1,2,0:T(8,128)(2,1)S(1)} fusion(bf16[1024,2880]{0,1:T(8,128)(2,1)} %get-tuple-element.74, bf16[1024,256]{1,0:T(8,128)(2,1)S(1)} %copy-done), kind=kOutput, calls=%fused_computation.36 | convolution fusion | flops 1510686720 | bytes 7897088 | tf_op jit(solution)/shard_map/dot_general | solution.py:117
  235.5 4.4 %fusion.21 = bf16[1,256,2880]{1,2,0:T(8,128)(2,1)S(1)} fusion(bf16[1024,2880]{0,1:T(8,128)(2,1)} %copy-done.12, bf16[1024,256]{1,0:T(8,128)(2,1)S(1)} %copy-done), kind=kOutput, calls=%fused_computation.37 | convolution fusion | flops 1510686720 | bytes 7897088 | tf_op jit(solution)/shard_map/dot_general | solution.py:117
  239.8 1.9 pad_maximum_fusion
  241.7 28.6 %all-to-all-done.5 = f32[32,32,329]{2,1,0:T(8,128)S(1)} async-done(((f32[32,32,329]{2,1,0:T(8,128)}), f32[32,32,329]{2,1,0:T(8,128)S(1)}, u32[]{:S(2)}, u32[]{:S(2)}) %all-to-all-start.5) | async-done | bytes 1347616 | tf_op jit(solution)/shard_map/all_to_all | solution.py:46
  270.3 1.1 slice_multiply_fusion
  271.4 1.0 fusion.46
  272.3 0.9 copy.39
  (62 shorter events, 0.5 us)
Async XLA Ops:
  0.6 1.0 copy-start
  0.6 8.5 %copy-start.7 = (bf16[2,256,2880]{1,2,0:T(8,128)(2,1)S(1)}, bf16[2,256,2880]{1,2,0:T(8,128)(2,1)}, u32[]{:S(2)}) copy-start(bf16[2,256,2880]{1,2,0:T(8,128)(2,1)} %param.9) | copy-start | bytes 8847364
  0.7 8.5 %copy-start.11 = (f32[1024]{0:T(1024)S(1)}, f32[1024]{0:T(1024)}, u32[]{:S(2)}) copy-start(f32[1024]{0:T(1024)} %param.11) | copy-start | bytes 12292
  9.1 12.6 %copy-start.9 = (bf16[72,1024]{1,0:T(8,128)(2,1)S(1)}, bf16[72,1024]{1,0:T(8,128)(2,1)}, u32[]{:S(2)}) copy-start(bf16[72,1024]{1,0:T(8,128)(2,1)} %param.12) | copy-start | bytes 442372
  9.1 12.6 %copy-start.10 = (f32[72]{0:T(128)S(1)}, f32[72]{0:T(128)}, u32[]{:S(2)}) copy-start(f32[72]{0:T(128)} %param.13) | copy-start | bytes 868
  21.8 3.9 %copy-start.1 = (bf16[1024,2880]{0,1:T(8,128)(2,1)}, bf16[1024,2880]{0,1:T(8,128)(2,1)S(1)}, u32[]{:S(2)}) copy-start(bf16[1024,2880]{0,1:T(8,128)(2,1)S(1)} %get-tuple-element.71) | copy-start | bytes 17694724
  21.8 4.2 %copy-start.2 = (bf16[1024,2880]{0,1:T(8,128)(2,1)}, bf16[1024,2880]{0,1:T(8,128)(2,1)S(1)}, u32[]{:S(2)}) copy-start(bf16[1024,2880]{0,1:T(8,128)(2,1)S(1)} %get-tuple-element.70) | copy-start | bytes 17694724
  23.7 2.5 copy-start.3
  26.2 0.8 copy-start.5
  30.0 25.4 %all-to-all-start = ((bf16[2,72,2880]{1,0,2:T(2,128)(2,1)}), bf16[2,72,2880]{1,0,2:T(2,128)(2,1)S(1)}, u32[]{:S(2)}, u32[]{:S(2)}) async-start(bf16[2,72,2880]{1,0,2:T(2,128)(2,1)} %copy.34), calls=%async_computation | async-start | bytes 2949120 | tf_op jit(solution)/shard_map/all_to_all | solution.py:101
  107.4 15.2 %all-to-all-start.1 = ((f32[8,2,32,360]{3,2,1,0:T(8,128)}), f32[8,2,32,360]{3,2,1,0:T(8,128)S(1)}, u32[]{:S(2)}, u32[]{:S(2)}) async-start(f32[8,2,32,360]{3,2,1,0:T(8,128)} %split.8), calls=%async_computation.1 | async-start | bytes 1572864 | tf_op jit(solution)/shard_map/all_to_all | solution.py:34
  122.6 16.3 %all-to-all-start.2 = ((f32[8,2,40,360]{3,2,1,0:T(8,128)}), f32[8,2,40,360]{3,2,1,0:T(8,128)S(1)}, u32[]{:S(2)}, u32[]{:S(2)}) async-start(f32[8,2,40,360]{3,2,1,0:T(8,128)} %split.9), calls=%async_computation.2 | async-start | bytes 1966080 | tf_op jit(solution)/shard_map/all_to_all | solution.py:34
  126.3 14.9 %copy-start.4 = (bf16[1,72,2880]{2,1,0:T(8,128)(2,1)S(1)}, bf16[1,72,2880]{2,1,0:T(8,128)(2,1)}, u32[]{:S(2)}) copy-start(bf16[1,72,2880]{2,1,0:T(8,128)(2,1)} %copy-done.3) | copy-start | bytes 1244164
  126.3 14.9 %copy-start.6 = (bf16[1,72,2880]{2,1,0:T(8,128)(2,1)S(1)}, bf16[1,72,2880]{2,1,0:T(8,128)(2,1)}, u32[]{:S(2)}) copy-start(bf16[1,72,2880]{2,1,0:T(8,128)(2,1)} %copy-done.5) | copy-start | bytes 1244164
  141.3 14.3 %slice-start.2 = ((s8[5898240]{0:T(1024)(128)(4,1)}), s8[4194304]{0:T(1024)(128)(4,1)S(1)}, s32[]{:S(2)}) async-start(s8[5898240]{0:T(1024)(128)(4,1)} %bitcast.112), calls=%async_computation.8 | async-start | bytes 8388608
  141.3 15.5 %slice-start.4 = ((s8[11796480]{0:T(1024)(128)(4,1)}), s8[4194304]{0:T(1024)(128)(4,1)S(1)}, s32[]{:S(2)}) async-start(s8[11796480]{0:T(1024)(128)(4,1)} %bitcast.121), calls=%async_computation.10 | async-start | bytes 8388608
  143.6 12.0 %slice-start.3 = ((s8[5898240]{0:T(1024)(128)(4,1)}), s8[1703936]{0:T(1024)(128)(4,1)S(1)}, s32[]{:S(2)}) async-start(s8[5898240]{0:T(1024)(128)(4,1)} %bitcast.112), calls=%async_computation.9 | async-start | bytes 3407872
  143.6 13.2 %slice-start.5 = ((s8[11796480]{0:T(1024)(128)(4,1)}), s8[4194304]{0:T(1024)(128)(4,1)S(1)}, s32[]{:S(2)}) async-start(s8[11796480]{0:T(1024)(128)(4,1)} %bitcast.121), calls=%async_computation.11 | async-start | bytes 8388608
  143.6 13.2 %slice-start.6 = ((s8[11796480]{0:T(1024)(128)(4,1)}), s8[3407872]{0:T(1024)(128)(4,1)S(1)}, s32[]{:S(2)}) async-start(s8[11796480]{0:T(1024)(128)(4,1)} %bitcast.121), calls=%async_computation.12 | async-start | bytes 6815744
  155.5 11.7 %copy-start.12 = (bf16[1024,2880]{0,1:T(8,128)(2,1)}, bf16[1024,2880]{0,1:T(8,128)(2,1)S(1)}, u32[]{:S(2)}) copy-start(bf16[1024,2880]{0,1:T(8,128)(2,1)S(1)} %get-tuple-element.76) | copy-start | bytes 17694724
  155.6 13.5 %slice-start = ((s8[5898240]{0:T(1024)(128)(4,1)}), s8[4194304]{0:T(1024)(128)(4,1)S(1)}, s32[]{:S(2)}) async-start(s8[5898240]{0:T(1024)(128)(4,1)} %bitcast.110), calls=%async_computation.6 | async-start | bytes 8388608
  156.8 10.5 %copy-start.8 = (bf16[2,256,2880]{1,2,0:T(8,128)(2,1)S(1)}, bf16[2,256,2880]{1,2,0:T(8,128)(2,1)}, u32[]{:S(2)}) copy-start(bf16[2,256,2880]{1,2,0:T(8,128)(2,1)} %param.9) | copy-start | bytes 8847364
  156.8 12.3 %slice-start.1 = ((s8[5898240]{0:T(1024)(128)(4,1)}), s8[1703936]{0:T(1024)(128)(4,1)S(1)}, s32[]{:S(2)}) async-start(s8[5898240]{0:T(1024)(128)(4,1)} %bitcast.110), calls=%async_computation.7 | async-start | bytes 3407872
  223.9 46.3 %all-to-all-start.5 = ((f32[32,32,329]{2,1,0:T(8,128)}), f32[32,32,329]{2,1,0:T(8,128)S(1)}, u32[]{:S(2)}, u32[]{:S(2)}) async-start(f32[32,32,329]{2,1,0:T(8,128)} %broadcast_in_dim.12), calls=%async_computation.5 | async-start | bytes 3145728 | tf_op jit(solution)/shard_map/all_to_all | solution.py:46
where the time goes:
time: 274 us; the launch traced here: 273 us
  waiting for transfers between devices  66.9 us (24%)
  matrix products  64.1 us (23%)
  other arithmetic  57.3 us (21%)
  blocking collectives  46.4 us (17%)
  starting transfers between devices  20.6 us (8%)
  local copies, waits for them, and re-layouts  16.1 us (6%)
    add x16, other arithmetic, lone_realization(): return (total + slope(values - other.astype(jnp.float32)[None]), None)  48.1 us
    all_to_all x1, blocking collectives, sent_and_summed(): lax.all_to_all(split_up(array, dim, devices), axis, 0, 0, tiled=True)  36.3 us
    all_to_all x1, waiting for transfers between devices, copy_for_each(): lax.all_to_all(jnp.broadcast_to(array[None], (devices, *array.shape)), ax...  28.6 us
    dot_general x2, matrix products, on_device(): jnp.dot(w_out.T, prediction_adjoint, preferred_element_type=jnp.float32)  22.3 us
    dot_general x2, matrix products, on_device(): jnp.dot(w_in, hidden_codes[ensemble_position], preferred_element_type=jnp...  20.1 us
    all_to_all x1, waiting for transfers between devices, on_device(): lax.all_to_all(predicted_maps, 'member', split_axis=2, concat_axis=0, til...  19.4 us
    all_to_all x2, waiting for transfers between devices, exchange_in_pieces(): lax.all_to_all(piece, axis, split_axis=0, concat_axis=0, tiled=True)  18.9 us
    all_to_all x1, blocking collectives, copy_for_each(): lax.all_to_all(jnp.broadcast_to(array[None], (devices, *array.shape)), ax...  10 us
  transfers between devices with their start and end apart: 4, of which 4 were waited for; matrix products, arithmetic and copies ran while one was open for 6% of the time, Pallas kernels for 0%

commit v1 on v0

v1 whole, which is shorter than its diff:
```python
import math

import jax
import jax.numpy as jnp
from jax import lax
from jax.experimental import pallas as pl
from jax.experimental.pallas import tpu as pltpu
from jax.sharding import Mesh
from jax.sharding import PartitionSpec as P

LON = 1440
BLK = 768
SUB = 256
C0 = math.sqrt(2.0 / math.pi)
C1 = C0 * 0.044715
F32 = jnp.float32
BF16 = jnp.bfloat16

FINE = (("y", 4), ("xl", 2), ("z", 8), ("xh", 2), ("c", 2))
MEMBER = ("y", "xl")
SPACE = ("z", "xh", "c")
CHIPS = ("y", "xl", "z", "xh")


def fwd_kernel(cells, hc_ref, w_in_ref, b_ref, w_out_ref, bo_ref, f_ref, act_ref, gp_ref):
    hid = w_in_ref.shape[0]
    hc = hc_ref[0]
    lane = lax.broadcasted_iota(jnp.int32, hc.shape, 1) + pl.program_id(1) * BLK
    hc = jnp.where(lane < cells, hc, jnp.zeros_like(hc))
    for k in range(hid // SUB):
        rows = pl.ds(k * SUB, SUB)
        pre = jnp.dot(w_in_ref[rows, :], hc, preferred_element_type=F32)
        x = pre + jnp.concatenate([b_ref[rows, :]] * (BLK // 128), axis=1)
        x2 = x * x
        t = jnp.tanh(x * (C1 * x2 + C0))
        h = 0.5 * t + 0.5
        a = x * h
        g = a * (1.0 - h) * ((6.0 * C1) * x2 + 2.0 * C0) + h
        act_ref[0, rows, :] = a.astype(BF16)
        gp_ref[0, rows, :] = g.astype(BF16)
    f = jnp.dot(w_out_ref[...], act_ref[0], preferred_element_type=F32)
    f = (f + bo_ref[...]).astype(BF16)
    half = BLK // 2
    f_ref[0, 0] = f[:, :half]
    f_ref[1, 0] = f[:, half:]


def decoder_forward(hidden_codes, w_in, b_wide, w_out, b_out):
    members, latent, cells = hidden_codes.shape
    hid, chan = w_in.shape[0], w_out.shape[0]
    nblk = pl.cdiv(cells, BLK)
    pad = nblk * BLK
    return pl.pallas_call(
        lambda *refs: fwd_kernel(cells, *refs),
        grid=(members, nblk),
        in_specs=[
            pl.BlockSpec((1, latent, BLK), lambda m, j: (m, 0, j)),
            pl.BlockSpec((hid, latent), lambda m, j: (0, 0)),
            pl.BlockSpec((hid, 128), lambda m, j: (0, 0)),
            pl.BlockSpec((chan, hid), lambda m, j: (0, 0)),
            pl.BlockSpec((chan, 1), lambda m, j: (0, 0)),
        ],
        out_specs=[
            pl.BlockSpec((2, 1, chan, BLK // 2), lambda m, j: (j, m, 0, 0)),
            pl.BlockSpec((1, hid, BLK), lambda m, j: (m, 0, j)),
            pl.BlockSpec((1, hid, BLK), lambda m, j: (m, 0, j)),
        ],
        out_shape=[
            jax.ShapeDtypeStruct((2 * nblk, members, chan, BLK // 2), BF16),
            jax.ShapeDtypeStruct((members, hid, pad), BF16),
            jax.ShapeDtypeStruct((members, hid, pad), BF16),
        ],
        compiler_params=pltpu.CompilerParams(dimension_semantics=("arbitrary", "arbitrary")),
        name="decoder_forward",
    )(hidden_codes, w_in, b_wide, w_out, b_out)


def slope(d):
    return d * lax.rsqrt(d * d + 0.0625)


def pair_kernel(cells, me_ref, area_ref, f_ref, t_ref, d_ref):
    groups, local, chan, wide = f_ref.shape
    members = groups * local
    me = me_ref[0]

    def strip(i, carry):
        rows = pl.ds(pl.multiple_of(i * 8, 8), 8)
        for l in range(wide // 128):
            lanes = pl.ds(l * 128, 128)
            v = [f_ref[m // local, m % local, rows, lanes].astype(F32) for m in range(members)]
            total = [None] * members
            for m in range(members):
                for q in range(m + 1, members):
                    s = slope(v[m] - v[q])
                    total[m] = s if total[m] is None else total[m] + s
                    total[q] = -s if total[q] is None else total[q] - s
            goal = t_ref[rows, lanes].astype(F32)
            cell = lax.broadcasted_iota(jnp.int32, (8, 128), 1) + (me * wide + l * 128)
            area = jnp.where(cell < LON, area_ref[0], area_ref[1])
            for m in range(members):
                d = area * (slope(v[m] - goal) - total[m] * (1.0 / members))
                d = jnp.where(cell < cells, d, 0.0)
                d_ref[m // local, m % local, rows, lanes] = d.astype(BF16)
        return carry

    lax.fori_loop(0, chan // 8, strip, 0)


def pair_gradient(me, area, block, target):
    groups, local, chan, wide = block.shape
    cells = target.shape[1]
    return pl.pallas_call(
        lambda *refs: pair_kernel(cells, *refs),
        grid_spec=pltpu.PrefetchScalarGridSpec(
            num_scalar_prefetch=2,
            grid=(1,),
            in_specs=[
                pl.BlockSpec(block.shape, lambda i, me, area: (0, 0, 0, 0)),
                pl.BlockSpec((chan, wide), lambda i, me, area: (0, me[0])),
            ],
            out_specs=pl.BlockSpec(block.shape, lambda i, me, area: (0, 0, 0, 0)),
        ),
        out_shape=jax.ShapeDtypeStruct(block.shape, BF16),
        name="pair_gradient",
    )(me, area, block, target)


def bwd_kernel(cells, d_ref, act_ref, gp_ref, hc_ref, w_out_t_ref, w_in_t_ref, cs_ref, g_ref, dpre_ref):
    hid = dpre_ref.shape[0]
    latent = hc_ref.shape[1]
    chan = d_ref.shape[2]
    nt = (((1,), (1,)), ((), ()))
    first = (pl.program_id(0) == 0) & (pl.program_id(1) == 0)

    @pl.when(first)
    def _():
        g_ref[...] = jnp.zeros_like(g_ref)

    hc = hc_ref[0]
    lane = lax.broadcasted_iota(jnp.int32, hc.shape, 1) + pl.program_id(1) * BLK
    hc = jnp.where(lane < cells, hc, jnp.zeros_like(hc))
    d = jnp.concatenate([d_ref[0, 0], d_ref[1, 0]], axis=1)
    d = jnp.concatenate([d, jnp.zeros((128 - chan, BLK), BF16)], axis=0)
    bias_lane = lax.broadcasted_iota(jnp.int32, (SUB, 128), 1) == chan
    for k in range(hid // SUB):
        rows = pl.ds(k * SUB, SUB)
        dact = jnp.dot(w_out_t_ref[rows, :], d, preferred_element_type=F32)
        dpre = dact * gp_ref[0, rows, :].astype(F32)
        dpre_b = dpre.astype(BF16)
        dpre_ref[rows, :] = dpre_b
        part = dpre[:, :128]
        for l in range(1, BLK // 128):
            part = part + dpre[:, l * 128 : (l + 1) * 128]
        bias = jnp.sum(part, axis=1, keepdims=True)
        g_ref[rows, :latent] += lax.dot_general(dpre_b, hc, nt, preferred_element_type=F32)
        out = lax.dot_general(act_ref[0, rows, :], d, nt, preferred_element_type=F32)
        g_ref[rows, latent:] += jnp.where(bias_lane, bias, out)
    cs = jnp.dot(w_in_t_ref[...], dpre_ref[...], preferred_element_type=F32)
    cs_ref[0] = cs.astype(BF16)


def decoder_backward(dfor, act, gp, hidden_codes, w_out_t, w_in_t):
    members, latent, cells = hidden_codes.shape
    hid = act.shape[1]
    chan = dfor.shape[2]
    nblk = pl.cdiv(cells, BLK)
    return pl.pallas_call(
        lambda *refs: bwd_kernel(cells, *refs),
        grid=(members, nblk),
        in_specs=[
            pl.BlockSpec((2, 1, chan, BLK // 2), lambda m, j: (j, m, 0, 0)),
            pl.BlockSpec((1, hid, BLK), lambda m, j: (m, 0, j)),
            pl.BlockSpec((1, hid, BLK), lambda m, j: (m, 0, j)),
            pl.BlockSpec((1, latent, BLK), lambda m, j: (m, 0, j)),
            pl.BlockSpec((hid, 128), lambda m, j: (0, 0)),
            pl.BlockSpec((latent, hid), lambda m, j: (0, 0)),
        ],
        out_specs=[
            pl.BlockSpec((1, latent, BLK), lambda m, j: (m, 0, j)),
            pl.BlockSpec((hid, latent + 128), lambda m, j: (0, 0)),
        ],
        out_shape=[
            jax.ShapeDtypeStruct((members, latent, cells), BF16),
            jax.ShapeDtypeStruct((hid, latent + 128), F32),
        ],
        scratch_shapes=[pltpu.VMEM((hid, BLK), BF16)],
        compiler_params=pltpu.CompilerParams(dimension_semantics=("arbitrary", "arbitrary")),
        name="decoder_backward",
    )(dfor, act, gp, hidden_codes, w_out_t, w_in_t)


def total_gradient(grads, scale):
    hid, wide = grads.shape
    half = hid // 2
    chips = lax.axis_size(CHIPS)
    core = lax.axis_index("c")
    swap = [(0, 1), (1, 0)]
    keep = lax.dynamic_slice(grads, (core * half, 0), (half, wide))
    give = lax.dynamic_slice(grads, ((1 - core) * half, 0), (half, wide)).astype(BF16)
    both = keep + lax.ppermute(give, "c", swap).astype(F32)
    shares = both.astype(BF16).reshape(chips, half // chips, wide)
    shares = lax.all_to_all(shares, CHIPS, 0, 0, tiled=True)
    share = (jnp.sum(shares.astype(F32), axis=0) * scale).astype(BF16)
    mine = lax.all_to_all(
        jnp.broadcast_to(share[None], (chips, *share.shape)), CHIPS, 0, 0, tiled=True
    ).reshape(half, wide)
    other = lax.ppermute(mine, "c", swap)
    low = jnp.where(core == 0, mine, other)
    high = jnp.where(core == 0, other, mine)
    return jnp.concatenate([low, high], axis=0).astype(F32)


def on_device(hidden_codes, w_in, b_in, w_out, b_out, target, band_start):
    local, latent, cells = hidden_codes.shape
    chan = w_out.shape[0]
    rows = cells // LON
    lat_rows = rows * lax.axis_size(SPACE)
    members = local * lax.axis_size(MEMBER)
    angle = ((band_start[0] + jnp.arange(rows, dtype=jnp.int32)).astype(F32) + 0.5) * (
        math.pi / lat_rows
    ) - math.pi / 2
    area = jnp.cos(angle)
    me = lax.axis_index(MEMBER).astype(jnp.int32).reshape(1)
    b_wide = jnp.broadcast_to(b_in[:, None], (b_in.shape[0], 128))
    w_out_t = jnp.pad(w_out.T, ((0, 0), (0, 128 - chan)))
    forecast, act, gp = decoder_forward(hidden_codes, w_in, b_wide, w_out, b_out[:, None])
    block = lax.all_to_all(forecast, MEMBER, 0, 0, tiled=True)
    dfor = pair_gradient(me, area, block, target)
    dfor = lax.all_to_all(dfor, MEMBER, 0, 0, tiled=True)
    code_sensitivity, grads = decoder_backward(dfor, act, gp, hidden_codes, w_out_t, w_in.T)
    total = total_gradient(grads, 1.0 / math.sqrt(members * cells))
    return (
        code_sensitivity,
        total[:, :latent],
        total[:, latent : latent + chan].T,
        total[:, latent + chan],
    )


def solution(mesh):
    fine = Mesh(mesh.devices.reshape([n for _, n in FINE]), [a for a, _ in FINE])
    in_specs = (P(MEMBER, None, SPACE), P(), P(), P(), P(), P(None, SPACE), P(SPACE))
    out_specs = (P(MEMBER, None, SPACE), P(), P(), P())
    return jax.shard_map(
        on_device, mesh=fine, in_specs=in_specs, out_specs=out_specs, check_vma=False
    )
```

time: 274 us -> 160 us (0.58)
  matrix products: 64.1 us -> 0 us
  other arithmetic: 57.3 us -> 3.14 us
  Pallas kernels: 0 us -> 46.9 us
  waiting for transfers between devices: 66.9 us -> 23.4 us
  starting transfers between devices: 20.6 us -> 16.5 us
  blocking collectives: 46.4 us -> 49.9 us
    dot_general x12 -> x0, matrix products: 64.1 us -> none  [the longest x2 22.3 us: on_device(): jnp.dot(w_out.T, prediction_adjoint, preferred_element_type=jnp.float32)]
    add x16 -> x0, other arithmetic: 48.1 us -> none  [lone_realization(): return (total + slope(values - other.astype(jnp.float32)[None]), None)]
    pallas_call x0 -> x3, Pallas kernels: none -> 46.9 us  [the longest x1 20.6 us: decoder_backward(): pl.pallas_call(lambda *refs: bwd_kernel(cells, *refs), grid=(members, nbl...]
    all_to_all x4 -> x2, waiting for transfers between devices: 66.9 us -> 22.1 us  [the longest x1 11.6 us: on_device(): block = lax.all_to_all(forecast, MEMBER, 0, 0, tiled=True)]
    all_to_all x4 -> x2, starting transfers between devices: 20.6 us -> 10 us  [the longest x1 5.94 us: on_device(): block = lax.all_to_all(forecast, MEMBER, 0, 0, tiled=True)]
    unnamed x41 -> x21, local copies, waits for them, and re-layouts: 3.26 us -> 11.3 us
    ppermute x0 -> x2, starting transfers between devices: none -> 6.51 us  [the longest x1 3.91 us: total_gradient(): other = lax.ppermute(mine, 'c', swap)]
    split x2 -> x0, local copies, waits for them, and re-layouts: 4.28 us -> none  [exchange_in_pieces(): jnp.split(parts, edges_of(parts.shape[cut], pieces), axis=cut)]
  transfers between devices with their start and end apart: 4 -> 4, of which waited for: 4 -> 3; matrix products, arithmetic and copies ran while one was open for 6% -> 3% of each run, Pallas kernels for 0% -> 0%
where the time goes in v1:
time: 160 us; the launch traced here: 159 us
  blocking collectives  49.9 us (31%)
  Pallas kernels  46.9 us (29%)
  waiting for transfers between devices  23.4 us (15%)
  local copies, waits for them, and re-layouts  18 us (11%)
  starting transfers between devices  16.5 us (10%)
  other arithmetic  3.14 us (2%)
    all_to_all x1, blocking collectives, total_gradient(): shares = lax.all_to_all(shares, CHIPS, 0, 0, tiled=True)  27.8 us
    all_to_all x1, blocking collectives, total_gradient(): lax.all_to_all(jnp.broadcast_to(share[None], (chips, *share.shape)), CHIP...  22 us
    pallas_call x1, Pallas kernels, decoder_backward(): pl.pallas_call(lambda *refs: bwd_kernel(cells, *refs), grid=(members, nbl...  20.6 us
    pallas_call x1, Pallas kernels, decoder_forward(): pl.pallas_call(lambda *refs: fwd_kernel(cells, *refs), grid=(members, nbl...  19.6 us
    all_to_all x1, waiting for transfers between devices, on_device(): block = lax.all_to_all(forecast, MEMBER, 0, 0, tiled=True)  11.6 us
    unnamed x21, local copies, waits for them, and re-layouts  11.3 us
    all_to_all x1, waiting for transfers between devices, on_device(): dfor = lax.all_to_all(dfor, MEMBER, 0, 0, tiled=True)  10.4 us
    pallas_call x1, Pallas kernels, pair_gradient(): pl.pallas_call(lambda *refs: pair_kernel(cells, *refs), grid_spec=pltpu.P...  6.64 us
  transfers between devices with their start and end apart: 4, of which 3 were waited for; matrix products, arithmetic and copies ran while one was open for 3% of the time, Pallas kernels for 0%

profile of v1, /device:TPU:1, one launch (start us, length us, event | category | flops | bytes accessed | tf_op | source)
XLA Modules:
  0.0 159.2 jit_solution(668333848943878613)
XLA Ops:
  0.6 0.0 copy-start.7
  0.6 0.0 copy-start.6
  0.7 4.7 %copy.25.refs_0_.refs_3_ = bf16[2,256,2880]{2,1,0:T(8,128)(2,1)} copy(bf16[2,256,2880]{1,2,0:T(8,128)(2,1)} %param.7) | data formatting | bytes 5898240 | tf_op args[0]
  5.3 0.0 copy-done.7
  5.3 0.7 copy.26.refs_4_
  6.0 0.0 copy-done.6
  6.0 1.0 broadcast_in_dim.6.refs_2_
  7.0 19.6 %decoder_forward.1 = (bf16[8,2,72,384]{3,2,1,0:T(8,128)(2,1)}, bf16[2,1024,3072]{2,1,0:T(8,128)(2,1)}, bf16[2,1024,3072]{2,1,0:T(8,128)(2,1)}) custom-call(bf16[2,256,2880]{2,1,0:T(8,128)(2,1)} %copy.25.refs_0_.refs_3_, bf16[1024,256]{1,0:T(8,128)(2,1)} %refs_1_.1, f32[1024,128]{1,0:T(8,128)} %broadcast_in_dim.6.refs_2_, bf16[72,1024]{1,0:T(8,128)(2,1)} %refs_3_.3, ...), custom_call_target="tpu_custom_call" | custom-call | tf_op jit(solution)/shard_map/decoder_forward/pallas_call | solution.py:53
  26.7 5.9 %all-to-all-start = ((bf16[8,2,72,384]{3,2,1,0:T(8,128)(2,1)}), bf16[8,2,72,384]{3,2,1,0:T(8,128)(2,1)S(1)}, u32[]{:S(2)}, u32[]{:S(2)}) async-start(bf16[8,2,72,384]{3,2,1,0:T(8,128)(2,1)} %get-tuple-element.9), calls=%async_computation | async-start | bytes 1769472 | tf_op jit(solution)/shard_map/all_to_all | solution.py:228
  33.2 0.5 add_cosine_fusion.refs_1_
  33.8 11.6 %all-to-all-done.refs_2_ = bf16[8,2,72,384]{3,2,1,0:T(8,128)(2,1)S(1)} async-done(((bf16[8,2,72,384]{3,2,1,0:T(8,128)(2,1)}), bf16[8,2,72,384]{3,2,1,0:T(8,128)(2,1)S(1)}, u32[]{:S(2)}, u32[]{:S(2)}) %all-to-all-start) | async-done | bytes 884768 | tf_op jit(solution)/shard_map/all_to_all | solution.py:228
  45.4 0.0 copy-start
  45.4 0.9 copy-done
  46.3 0.0 copy-start.5
  46.3 6.6 %pair_gradient.1 = bf16[8,2,72,384]{3,2,1,0:T(8,128)(2,1)} custom-call(s32[1]{0:T(128)} %bitcast.refs_0_, f32[2]{0:T(128)} %add_cosine_fusion.refs_1_, bf16[8,2,72,384]{3,2,1,0:T(8,128)(2,1)} %copy-done, bf16[72,2880]{1,0:T(8,128)(2,1)} %refs_3_.4), custom_call_target="tpu_custom_call" | custom-call | tf_op jit(solution)/shard_map/pair_gradient/pallas_call | solution.py:113
  52.9 0.0 copy-start.3
  52.9 4.1 %all-to-all-start.1 = ((bf16[8,2,72,384]{3,2,1,0:T(8,128)(2,1)}), bf16[8,2,72,384]{3,2,1,0:T(8,128)(2,1)S(1)}, u32[]{:S(2)}, u32[]{:S(2)}) async-start(bf16[8,2,72,384]{3,2,1,0:T(8,128)(2,1)} %pair_gradient.1), calls=%async_computation.1 | async-start | bytes 1769472 | tf_op jit(solution)/shard_map/all_to_all | solution.py:230
  57.0 0.0 copy-done.5
  57.0 0.2 copy.27
  57.2 0.0 copy-done.3
  57.2 1.0 copy.28
  58.2 0.8 pad.4.refs_4_
  59.0 10.4 %all-to-all-done.1.refs_0_ = bf16[8,2,72,384]{3,2,1,0:T(8,128)(2,1)S(1)} async-done(((bf16[8,2,72,384]{3,2,1,0:T(8,128)(2,1)}), bf16[8,2,72,384]{3,2,1,0:T(8,128)(2,1)S(1)}, u32[]{:S(2)}, u32[]{:S(2)}) %all-to-all-start.1) | async-done | bytes 884768 | tf_op jit(solution)/shard_map/all_to_all | solution.py:230
  69.4 0.0 copy-start.1
  69.4 0.9 copy-done.1
  70.3 20.6 %decoder_backward.1 = (bf16[2,256,2880]{2,1,0:T(8,128)(2,1)}, f32[1024,384]{1,0:T(8,128)}) custom-call(bf16[8,2,72,384]{3,2,1,0:T(8,128)(2,1)} %copy-done.1, bf16[2,1024,3072]{2,1,0:T(8,128)(2,1)} %get-tuple-element.10.refs_1_, bf16[2,1024,3072]{2,1,0:T(8,128)(2,1)} %get-tuple-element.11.refs_2_, bf16[2,256,2880]{2,1,0:T(8,128)(2,1)} %copy.25.refs_0_.refs_3_, ...), custom_call_target="tpu_custom_call" | custom-call | tf_op jit(solution)/shard_map/decoder_backward/pallas_call | solution.py:168
  90.9 1.2 dynamic-slice_convert_fusion
  92.1 2.6 %collective-permute-start = (bf16[512,384]{1,0:T(8,128)(2,1)S(1)}, bf16[512,384]{1,0:T(8,128)(2,1)S(1)}, u32[]{:S(2)}, u32[]{:S(2)}) collective-permute-start(bf16[512,384]{1,0:T(8,128)(2,1)S(1)} %dynamic-slice_convert_fusion), channel_id=1, source_target_pairs={{0,1},{1,0},{2,3},{3,2},{4,5},{5,4},{6,7},{7,6},{8,9},{9,8},{10,11... | collective-permute-start | bytes 1179656 | tf_op jit(solution)/shard_map/ppermute | solution.py:201
  94.7 1.3 collective-permute-done
  96.1 1.2 add_convert_fusion
  97.3 0.1 reshape.23
  97.4 0.0 copy-start.2
  97.4 27.8 %all_to_all.20 = bf16[128,4,384]{2,1,0:T(4,128)(2,1)S(1)} all-to-all(bf16[128,4,384]{2,1,0:T(4,128)(2,1)S(1)} %reshape.23), channel_id=1, replica_groups=mesh['y'=4,'xl'=2,'z'=8,'xh'=2,'c'=2] {'y','xl','z','xh'}, dimensions={0} | all-to-all | bytes 786432 | tf_op jit(solution)/shard_map/all_to_all | solution.py:203
  125.2 0.2 convert_reduce_fusion
  125.5 0.1 broadcast_in_dim.8
  125.6 22.0 %all_to_all.21 = bf16[128,4,384]{2,1,0:T(4,128)(2,1)S(1)} all-to-all(bf16[128,4,384]{2,1,0:T(4,128)(2,1)S(1)} %broadcast_in_dim.8), channel_id=1, replica_groups=mesh['y'=4,'xl'=2,'z'=8,'xh'=2,'c'=2] {'y','xl','z','xh'}, dimensions={0} | all-to-all | bytes 786432 | tf_op jit(solution)/shard_map/all_to_all | solution.py:205
  147.6 0.8 reshape.24
  148.4 3.9 %collective-permute-start.1 = (bf16[512,384]{1,0:T(8,128)(2,1)}, bf16[512,384]{1,0:T(8,128)(2,1)}, u32[]{:S(2)}, u32[]{:S(2)}) collective-permute-start(bf16[512,384]{1,0:T(8,128)(2,1)} %reshape.24), channel_id=1, source_target_pairs={{0,1},{1,0},{2,3},{3,2},{4,5},{5,4},{6,7},{7,6},{8,9},{9,8},{10,11... | collective-permute-start | bytes 1179656 | tf_op jit(solution)/shard_map/ppermute | solution.py:208
  152.4 0.0 copy-done.2
  152.4 0.0 copy-start.4
  152.4 2.7 %copy.30 = bf16[2,256,2880]{1,2,0:T(8,128)(2,1)} copy(bf16[2,256,2880]{2,1,0:T(8,128)(2,1)S(1)} %copy-done.2) | data formatting | bytes 5898240
  155.1 0.0 collective-permute-done.1
  155.1 0.0 copy-done.4
  155.1 1.1 broadcast_select_fusion.1
  156.2 0.1 maximum_convert_fusion
  156.3 1.1 slice.12
  157.4 1.0 slice_reduce_fusion
  158.3 0.9 copy.31
  (2 shorter events, 0.0 us)
Async XLA Ops:
  0.6 4.7 %copy-start.7 = (f32[72]{0:T(128)S(1)}, f32[72]{0:T(128)}, u32[]{:S(2)}) copy-start(f32[72]{0:T(128)} %param.11) | copy-start | bytes 868
  0.6 5.4 %copy-start.6 = (f32[1024]{0:T(1024)S(1)}, f32[1024]{0:T(1024)}, u32[]{:S(2)}) copy-start(f32[1024]{0:T(1024)} %param.9) | copy-start | bytes 12292
  26.7 18.7 %all-to-all-start = ((bf16[8,2,72,384]{3,2,1,0:T(8,128)(2,1)}), bf16[8,2,72,384]{3,2,1,0:T(8,128)(2,1)S(1)}, u32[]{:S(2)}, u32[]{:S(2)}) async-start(bf16[8,2,72,384]{3,2,1,0:T(8,128)(2,1)} %get-tuple-element.9), calls=%async_computation | async-start | bytes 1769472 | tf_op jit(solution)/shard_map/all_to_all | solution.py:228
  45.4 0.9 copy-start
  46.3 10.7 %copy-start.5 = (bf16[72,1024]{1,0:T(8,128)(2,1)S(1)}, bf16[72,1024]{1,0:T(8,128)(2,1)}, u32[]{:S(2)}) copy-start(bf16[72,1024]{1,0:T(8,128)(2,1)} %refs_3_.3) | copy-start | bytes 442372
  52.9 4.3 %copy-start.3 = (bf16[1024,256]{1,0:T(8,128)(2,1)S(1)}, bf16[1024,256]{1,0:T(8,128)(2,1)}, u32[]{:S(2)}) copy-start(bf16[1024,256]{1,0:T(8,128)(2,1)} %refs_1_.1) | copy-start | bytes 1572868
  52.9 16.5 %all-to-all-start.1 = ((bf16[8,2,72,384]{3,2,1,0:T(8,128)(2,1)}), bf16[8,2,72,384]{3,2,1,0:T(8,128)(2,1)S(1)}, u32[]{:S(2)}, u32[]{:S(2)}) async-start(bf16[8,2,72,384]{3,2,1,0:T(8,128)(2,1)} %pair_gradient.1), calls=%async_computation.1 | async-start | bytes 1769472 | tf_op jit(solution)/shard_map/all_to_all | solution.py:230
  69.4 0.9 copy-start.1
  92.1 4.0 %collective-permute-start = (bf16[512,384]{1,0:T(8,128)(2,1)S(1)}, bf16[512,384]{1,0:T(8,128)(2,1)S(1)}, u32[]{:S(2)}, u32[]{:S(2)}) collective-permute-start(bf16[512,384]{1,0:T(8,128)(2,1)S(1)} %dynamic-slice_convert_fusion), channel_id=1, source_target_pairs={{0,1},{1,0},{2,3},{3,2},{4,5},{5,4},{6,7},{7,6},{8,9},{9,8},{10,11... | collective-permute-start | bytes 1179656 | tf_op jit(solution)/shard_map/ppermute | solution.py:201
  97.4 55.0 %copy-start.2 = (bf16[2,256,2880]{2,1,0:T(8,128)(2,1)S(1)}, bf16[2,256,2880]{2,1,0:T(8,128)(2,1)}, u32[]{:S(2)}) copy-start(bf16[2,256,2880]{2,1,0:T(8,128)(2,1)} %get-tuple-element.22) | copy-start | bytes 8847364
  148.4 6.6 %collective-permute-start.1 = (bf16[512,384]{1,0:T(8,128)(2,1)}, bf16[512,384]{1,0:T(8,128)(2,1)}, u32[]{:S(2)}, u32[]{:S(2)}) collective-permute-start(bf16[512,384]{1,0:T(8,128)(2,1)} %reshape.24), channel_id=1, source_target_pairs={{0,1},{1,0},{2,3},{3,2},{4,5},{5,4},{6,7},{7,6},{8,9},{9,8},{10,11... | collective-permute-start | bytes 1179656 | tf_op jit(solution)/shard_map/ppermute | solution.py:208
  152.4 2.7 %copy-start.4 = (bf16[512,384]{1,0:T(8,128)(2,1)S(1)}, bf16[512,384]{1,0:T(8,128)(2,1)}, u32[]{:S(2)}) copy-start(bf16[512,384]{1,0:T(8,128)(2,1)} %reshape.24) | copy-start | bytes 1179652

commit v2 on v1

v2 whole, which is shorter than its diff:
```python
import math

import jax
import jax.numpy as jnp
from jax import lax
from jax.experimental import pallas as pl
from jax.experimental.pallas import tpu as pltpu
from jax.sharding import Mesh
from jax.sharding import PartitionSpec as P

LON = 1440
PER = 360
BLK = 2 * PER
BBLK = 4 * PER
SUB = 256
FSUB = 512
C0 = math.sqrt(2.0 / math.pi)
C1 = C0 * 0.044715
F32 = jnp.float32
BF16 = jnp.bfloat16
NT = (((1,), (1,)), ((), ()))

FINE = (("y", 4), ("xl", 2), ("z", 8), ("xh", 2), ("c", 2))
MEMBER = ("y", "xl")
SPACE = ("z", "xh", "c")
PLANE = ("y", "xl", "xh")


VMEM = pl.BlockSpec(memory_space=pltpu.VMEM)
SMEM = pl.BlockSpec(memory_space=pltpu.SMEM)


def on_chip(x):
    return pltpu.with_memory_space_constraint(x, pltpu.VMEM)


def limit(mib):
    return pltpu.CompilerParams(vmem_limit_bytes=mib * 2**20)


def whole(shape):
    return pl.BlockSpec(shape, lambda *a: (0,) * len(shape))


def halved(w):
    return (w.astype(F32) * 0.5).astype(BF16)


def column(row):
    return jnp.broadcast_to(row, (128, row.shape[1])).T


def fwd_kernel(hc_ref, w_in_ref, b_ref, w_out_ref, bo_ref, f_ref, wide_ref):
    hid = w_in_ref.shape[0]
    cells = hc_ref.shape[1]
    for i in range(hid // 128):
        rows = pl.ds(i * 128, 128)
        wide_ref[rows, :] = column(b_ref[:, rows])
    hc = hc_ref[0]
    half_out = halved(w_out_ref[...])
    f = None
    for k in range(hid // FSUB):
        rows = pl.ds(k * FSUB, FSUB)
        pre = lax.dot_general(w_in_ref[rows, :], hc, NT, preferred_element_type=F32)
        b = jnp.concatenate([wide_ref[rows, :]] * pl.cdiv(cells, 128), axis=1)[:, :cells]
        x = pre + b
        t = jnp.tanh(x * (C1 * (x * x) + C0))
        act = (x * (t + 1.0)).astype(BF16)
        part = jnp.dot(half_out[:, k * FSUB : (k + 1) * FSUB], act, preferred_element_type=F32)
        f = part if f is None else f + part
    f = (f + column(bo_ref[...])[:, :1]).astype(BF16)
    for i in range(cells // PER):
        f_ref[i, 0] = f[:, i * PER : (i + 1) * PER]


def decoder_forward(codes, w_in, b_in, w_out, b_out):
    members, cells, latent = codes.shape
    hid, chan = w_in.shape[0], w_out.shape[0]
    groups = cells // PER
    return pl.pallas_call(
        fwd_kernel,
        grid=(members,),
        in_specs=[
            pl.BlockSpec((1, cells, latent), lambda m: (m, 0, 0)),
            whole(w_in.shape),
            whole(b_in.shape),
            whole(w_out.shape),
            whole(b_out.shape),
        ],
        out_specs=pl.BlockSpec((groups, 1, chan, PER), lambda m: (0, m, 0, 0)),
        out_shape=jax.ShapeDtypeStruct((groups, members, chan, PER), BF16),
        scratch_shapes=[pltpu.VMEM((hid, 128), F32)],
        compiler_params=pltpu.CompilerParams(dimension_semantics=("arbitrary",)),
        name="decoder_forward",
    )(codes, w_in, b_in, w_out, b_out)


def gate_kernel(hc_ref, w_in_ref, b_ref, *refs):
    act_ref, gp_ref = refs[-2:]
    hid = w_in_ref.shape[0]
    hc = hc_ref[0]
    for k in range(hid // SUB):
        rows = pl.ds(k * SUB, SUB)
        pre = lax.dot_general(hc, w_in_ref[rows, :], NT, preferred_element_type=F32)
        x = pre + b_ref[:, rows]
        x2 = x * x
        t = jnp.tanh(x * (C1 * x2 + C0))
        p = t + 1.0
        a = x * p
        act_ref[0, :, rows] = a.astype(BF16)
        gp_ref[0, :, rows] = a * (1.0 - t) * ((3.0 * C1) * x2 + C0) + p


def decoder_gates(member, codes, w_in, b_in, so_far=()):
    members, cells, latent = codes.shape
    hid = w_in.shape[0]
    return pl.pallas_call(
        gate_kernel,
        grid=(cells // BLK,),
        in_specs=[
            pl.BlockSpec((1, BLK, latent), lambda j: (member, j, 0)),
            whole(w_in.shape),
            whole(b_in.shape),
        ]
        + [pl.BlockSpec(memory_space=pl.ANY)] * len(so_far),
        out_specs=[pl.BlockSpec((1, BLK, hid), lambda j: (member, j, 0))] * 2,
        out_shape=[
            jax.ShapeDtypeStruct((members, cells, hid), BF16),
            jax.ShapeDtypeStruct((members, cells, hid), F32),
        ],
        input_output_aliases={3 + i: i for i in range(len(so_far))},
        compiler_params=pltpu.CompilerParams(dimension_semantics=("arbitrary",)),
        cost_estimate=pl.CostEstimate(flops=8 * 10**9, transcendentals=3 * 10**6, bytes_accessed=20 * 10**6),
        name=f"decoder_gates_{member}",
    )(codes, w_in, b_in, *so_far)


def slope(d):
    return d * lax.rsqrt(d * d + 0.0625)


def pair_kernel(me_ref, area_ref, f_ref, t_ref, d_ref):
    groups, local, chan, wide = f_ref.shape
    members = groups * local
    me = me_ref[0]

    def strip(i, carry):
        rows = pl.ds(pl.multiple_of(i * 8, 8), 8)
        for l in range(0, wide, 128):
            n = min(128, wide - l)
            lanes = pl.ds(l, n)
            v = [f_ref[m // local, m % local, rows, lanes].astype(F32) for m in range(members)]
            total = [None] * members
            for m in range(members):
                for q in range(m + 1, members):
                    s = slope(v[m] - v[q])
                    total[m] = s if total[m] is None else total[m] + s
                    total[q] = -s if total[q] is None else total[q] - s
            goal = t_ref[rows, lanes].astype(F32)
            cell = lax.broadcasted_iota(jnp.int32, (8, n), 1) + (me * wide + l)
            area = jnp.where(cell < LON, area_ref[0], area_ref[1])
            for m in range(members):
                d = area * (slope(v[m] - goal) - total[m] * (1.0 / members))
                d_ref[m // local, m % local, rows, lanes] = d.astype(BF16)
        return carry

    lax.fori_loop(0, chan // 8, strip, 0)


def pair_gradient(me, area, block, goal):
    return pl.pallas_call(
        pair_kernel,
        in_specs=[SMEM, SMEM, VMEM, VMEM],
        out_specs=VMEM,
        out_shape=pltpu.VMEM(block.shape, BF16),
        compiler_params=limit(8),
        name="pair_gradient",
    )(me, area, on_chip(block), goal)


def bwd_kernel(d_ref, act_ref, gp_ref, hc_ref, w_out_ref, w_in_ref, cs_ref, g_ref, dpre_ref):
    hid, latent = w_in_ref.shape
    chan = w_out_ref.shape[0]
    first = (pl.program_id(0) == 0) & (pl.program_id(1) == 0)

    @pl.when(first)
    def _():
        g_ref[...] = jnp.zeros_like(g_ref)

    d = jnp.concatenate([d_ref[i, 0] for i in range(d_ref.shape[0])], axis=1)
    d_t = d.astype(F32).T.astype(BF16)
    hc_t = hc_ref[0].astype(F32).T.astype(BF16)
    left = jnp.concatenate([hc_t, jnp.ones((16, hc_t.shape[1]), BF16)], axis=0)
    half_out = halved(w_out_ref[...])
    bias_end = latent + 8

    def slab(k):
        cols = pl.ds(k * SUB, SUB)
        dact = jnp.dot(d_t, half_out[:, k * SUB : (k + 1) * SUB], preferred_element_type=F32)
        dpre_ref[:, cols] = (dact * gp_ref[0, :, cols]).astype(BF16)

    slab(0)
    for k in range(hid // SUB):
        if k + 1 < hid // SUB:
            slab(k + 1)
        cols = pl.ds(k * SUB, SUB)
        g_in = jnp.dot(left, dpre_ref[:, cols], preferred_element_type=F32)
        g_out = jnp.dot(d, act_ref[0, :, cols], preferred_element_type=F32)
        for i in range(SUB // 128):
            c = k * (SUB // 128) + i
            half, base = c // 4, (c % 4) * (bias_end + chan)
            lanes = slice(i * 128, (i + 1) * 128)
            g_ref[half, base : base + bias_end, :] += g_in[:bias_end, lanes]
            g_ref[half, base + bias_end : base + bias_end + chan, :] += g_out[:, lanes]
    cs = jnp.dot(dpre_ref[...], w_in_ref[...], preferred_element_type=F32)
    cs_ref[0] = cs.astype(BF16)


def decoder_backward(dfor, act, gp, codes, w_out, w_in):
    members, cells, latent = codes.shape
    hid = act.shape[2]
    chan = dfor.shape[2]
    rows = hid // 2 * (latent + 8 + chan) // 128
    return pl.pallas_call(
        bwd_kernel,
        grid=(members, cells // BBLK),
        in_specs=[
            pl.BlockSpec((BBLK // PER, 1, chan, PER), lambda m, j: (j, m, 0, 0)),
            pl.BlockSpec((1, BBLK, hid), lambda m, j: (m, j, 0)),
            pl.BlockSpec((1, BBLK, hid), lambda m, j: (m, j, 0)),
            pl.BlockSpec((1, BBLK, latent), lambda m, j: (m, j, 0)),
            whole(w_out.shape),
            whole(w_in.shape),
        ],
        out_specs=[
            pl.BlockSpec((1, BBLK, latent), lambda m, j: (m, j, 0)),
            whole((2, rows, 128)),
        ],
        out_shape=[
            jax.ShapeDtypeStruct((members, cells, latent), BF16),
            jax.ShapeDtypeStruct((2, rows, 128), F32),
        ],
        scratch_shapes=[pltpu.VMEM((BBLK, hid), BF16)],
        compiler_params=pltpu.CompilerParams(dimension_semantics=("arbitrary", "arbitrary")),
        name="decoder_backward",
    )(dfor, act, gp, codes, w_out, w_in)


def unpack_kernel(core_ref, mine_ref, other_ref, gi_ref, go_ref, gb_ref):
    chan = go_ref.shape[0]
    latent = gi_ref.shape[1]
    per = latent + 8 + chan
    lower = core_ref[0] == 0
    for c in range(8):
        rows = pl.ds((c % 4) * per, per)
        a, b = mine_ref[rows, :].astype(F32), other_ref[rows, :].astype(F32)
        x = jnp.where(lower == (c < 4), a, b)
        cols = slice(c * 128, (c + 1) * 128)
        gi_ref[cols, :] = x[:latent].T
        gb_ref[:, cols] = x[latent : latent + 1]
        go_ref[:, cols] = x[latent + 8 :] * 0.5


def unpack(core, mine, other, hid, latent, chan):
    return pl.pallas_call(
        unpack_kernel,
        in_specs=[SMEM, VMEM, VMEM],
        out_specs=[VMEM] * 3,
        out_shape=[
            jax.ShapeDtypeStruct((hid, latent), F32),
            jax.ShapeDtypeStruct((chan, hid), F32),
            jax.ShapeDtypeStruct((1, hid), F32),
        ],
        name="unpack_gradients",
    )(core, on_chip(mine), on_chip(other))


def total_gradient(grads, scale):
    _, rows, lanes = grads.shape
    plane = lax.axis_size(PLANE)
    per = -(-rows // (8 * plane)) * 8
    core = lax.axis_index("c")
    swap = [(0, 1), (1, 0)]
    keep = lax.dynamic_index_in_dim(grads, core, 0, keepdims=False)
    give = lax.dynamic_index_in_dim(grads, 1 - core, 0, keepdims=False).astype(BF16)
    both = (keep + lax.ppermute(give, "c", swap).astype(F32)).astype(BF16)
    both = jnp.pad(both, ((0, plane * per - rows), (0, 0))).reshape(plane, per, lanes)
    shares = lax.all_to_all(both, PLANE, 0, 0, tiled=True)
    share = jnp.sum(shares.astype(F32), axis=0)
    parts = lax.all_to_all(
        jnp.broadcast_to(share[None], (lax.axis_size("z"), *share.shape)), "z", 0, 0, tiled=True
    )
    share = (jnp.sum(parts, axis=0) * scale).astype(BF16)
    mine = lax.all_to_all(
        jnp.broadcast_to(share[None], (plane, *share.shape)), PLANE, 0, 0, tiled=True
    ).reshape(plane * per, lanes)[:rows]
    return mine, lax.ppermute(mine, "c", swap)


def on_device(hidden_codes, w_in, b_in, w_out, b_out, target, band_start):
    local, latent, cells = hidden_codes.shape
    hid, chan = w_in.shape[0], w_out.shape[0]
    rows = cells // LON
    lat_rows = rows * lax.axis_size(SPACE)
    members = local * lax.axis_size(MEMBER)
    angle = ((band_start[0] + jnp.arange(rows, dtype=jnp.int32)).astype(F32) + 0.5) * (
        math.pi / lat_rows
    ) - math.pi / 2
    area = jnp.cos(angle)
    me = lax.axis_index(MEMBER).astype(jnp.int32)
    codes = jnp.swapaxes(hidden_codes, 1, 2)
    b_row = b_in[None, :]
    forecast = decoder_forward(codes, w_in, b_row, w_out, b_out[None, :])
    block = lax.all_to_all(forecast, MEMBER, 0, 0, tiled=True)
    gates = decoder_gates(0, codes, w_in, b_row)
    goal = lax.dynamic_slice(target, (0, me * PER), (chan, PER))
    block, gates = lax.optimization_barrier((block, gates))
    dfor = pair_gradient(me.reshape(1), area, block, goal)
    dfor_in = lax.all_to_all(dfor, MEMBER, 0, 0, tiled=True)
    later_b, _ = lax.optimization_barrier((b_row, dfor))
    act, gp = decoder_gates(1, codes, w_in, later_b, gates)
    sensitivity, grads = decoder_backward(dfor_in, act, gp, codes, w_out, w_in)
    mine, other = total_gradient(grads, 1.0 / math.sqrt(members * cells))
    core = lax.axis_index("c").astype(jnp.int32).reshape(1)
    grad_in, grad_out, grad_b = unpack(core, mine, other, hid, latent, chan)
    return jnp.swapaxes(sensitivity, 1, 2), grad_in, grad_out, grad_b[0]


def solution(mesh):
    fine = Mesh(mesh.devices.reshape([n for _, n in FINE]), [a for a, _ in FINE])
    in_specs = (P(MEMBER, None, SPACE), P(), P(), P(), P(), P(None, SPACE), P(SPACE))
    out_specs = (P(MEMBER, None, SPACE), P(), P(), P())
    return jax.shard_map(
        on_device, mesh=fine, in_specs=in_specs, out_specs=out_specs, check_vma=False
    )
```

time: 160 us -> 129 us (0.81)
  waiting for transfers between devices: 23.4 us -> 6.18 us
  local copies, waits for them, and re-layouts: 18 us -> 2.27 us
  Pallas kernels: 46.9 us -> 57.3 us
  blocking collectives: 49.9 us -> 43.9 us
  other arithmetic: 3.14 us -> 1.3 us
    pallas_call x3 -> x6, Pallas kernels: 46.9 us -> 57.3 us  [the longest x2 20.7 us: decoder_gates(): pl.pallas_call(gate_kernel, grid=(cells // BLK,), in_specs=[pl.BlockSpec(...]
    unnamed x21 -> x4, local copies, waits for them, and re-layouts: 11.3 us -> 0.92 us
    all_to_all x1, waiting for transfers between devices: 11.6 us -> 1.58 us  [on_device(): block = lax.all_to_all(forecast, MEMBER, 0, 0, tiled=True)]
    all_to_all x1, waiting for transfers between devices: 10.4 us -> 2.04 us  [on_device(): dfor_in = lax.all_to_all(dfor, MEMBER, 0, 0, tiled=True)]
    all_to_all x2 -> x3, blocking collectives: 49.9 us -> 43.9 us  [the longest x1 19.2 us: total_gradient(): lax.all_to_all(jnp.broadcast_to(share[None], (lax.axis_size('z'), *share....]
    slice x2 -> x1, local copies, waits for them, and re-layouts: 2.01 us -> 0.02 us  [total_gradient(): lax.all_to_all(jnp.broadcast_to(share[None], (plane, *share.shape)), PLAN...]
    broadcast_in_dim x3 -> x2, local copies, waits for them, and re-layouts: 1.81 us -> 0.07 us  [the longest x1 0.05 us: total_gradient(): jnp.broadcast_to(share[None], (plane, *share.shape))]
  transfers between devices with their start and end apart: 4 -> 4, of which waited for: 3 -> 4; matrix products, arithmetic and copies ran while one was open for 3% -> 0% of each run, Pallas kernels for 0% -> 16%
where the time goes in v2:
time: 129 us
  Pallas kernels  57.3 us (44%)
  blocking collectives  43.9 us (34%)
  starting transfers between devices  16.7 us (13%)
  waiting for transfers between devices  6.18 us (5%)
  local copies, waits for them, and re-layouts  2.27 us (2%)
  between operations  1.36 us (1%)
  other arithmetic  1.3 us (1%)
    pallas_call x2, Pallas kernels, decoder_gates(): pl.pallas_call(gate_kernel, grid=(cells // BLK,), in_specs=[pl.BlockSpec(...  20.7 us
    all_to_all x1, blocking collectives, total_gradient(): lax.all_to_all(jnp.broadcast_to(share[None], (lax.axis_size('z'), *share....  19.2 us
    pallas_call x1, Pallas kernels, decoder_backward(): pl.pallas_call(bwd_kernel, grid=(members, cells // BBLK), in_specs=[pl.Bl...  18.9 us
    all_to_all x1, blocking collectives, total_gradient(): lax.all_to_all(jnp.broadcast_to(share[None], (plane, *share.shape)), PLAN...  12.6 us
    all_to_all x1, blocking collectives, total_gradient(): shares = lax.all_to_all(both, PLANE, 0, 0, tiled=True)  12.1 us
    pallas_call x1, Pallas kernels, decoder_forward(): pl.pallas_call(fwd_kernel, grid=(members,), in_specs=[pl.BlockSpec((1, ce...  11.2 us
    all_to_all x1, starting transfers between devices, on_device(): block = lax.all_to_all(forecast, MEMBER, 0, 0, tiled=True)  5.93 us
    pallas_call x1, Pallas kernels, pair_gradient(): pl.pallas_call(pair_kernel, in_specs=[SMEM, SMEM, VMEM, VMEM], out_specs=...  5.17 us
  transfers between devices with their start and end apart: 4, of which 4 were waited for; matrix products, arithmetic and copies ran while one was open for 0% of the time, Pallas kernels for 16%

profile of v2, /device:TPU:1, one launch (start us, length us, event | category | flops | bytes accessed | tf_op | source)
XLA Modules:
  0.0 129.0 jit_solution(7155739666977573250)
XLA Ops:
  0.6 0.0 copy-start
  0.6 11.2 %decoder_forward.1 = bf16[8,2,72,360]{3,2,1,0:T(8,128)(2,1)} custom-call(bf16[2,2880,256]{2,1,0:T(8,128)(2,1)} %bitcast.17, bf16[1024,256]{1,0:T(8,128)(2,1)} %w_in_ref.7, f32[1,1024]{1,0:T(1,128)} %bitcast.23, bf16[72,1024]{1,0:T(8,128)(2,1)} %w_out_ref.3, f32[1,72]{1,0:T(1,128)} %bitcast.26), custom_call_target="tpu_custom_call" | custom-call | tf_op jit(solution)/shard_map/decoder_forward/pallas_call | solution.py:80
  11.9 5.9 %all-to-all-start = ((bf16[8,2,72,360]{3,2,1,0:T(8,128)(2,1)}), bf16[8,2,72,360]{3,2,1,0:T(8,128)(2,1)S(1)}, u32[]{:S(2)}, u32[]{:S(2)}) async-start(bf16[8,2,72,360]{3,2,1,0:T(8,128)(2,1)} %decoder_forward.1), calls=%async_computation | async-start | bytes 1769472 | tf_op jit(solution)/shard_map/all_to_all | solution.py:314
  18.5 0.0 copy-done
  18.5 0.1 constant_dynamic-slice_fusion.t_ref
  18.6 10.4 %decoder_gates_0.1 = (bf16[2,2880,1024]{2,1,0:T(8,128)(2,1)}, f32[2,2880,1024]{2,1,0:T(8,128)}) custom-call(bf16[2,2880,256]{2,1,0:T(8,128)(2,1)} %bitcast.18, bf16[1024,256]{1,0:T(8,128)(2,1)} %w_in_ref.7, f32[1,1024]{1,0:T(1,128)} %bitcast.24), custom_call_target="tpu_custom_call" | custom-call | flops 8000000000 | bytes 20000000 | tf_op jit(solution)/shard_map/decoder_gates_0/pallas_call | solution.py:117
  29.0 1.6 %all-to-all-done.f_ref = bf16[8,2,72,360]{3,2,1,0:T(8,128)(2,1)S(1)} async-done(((bf16[8,2,72,360]{3,2,1,0:T(8,128)(2,1)}), bf16[8,2,72,360]{3,2,1,0:T(8,128)(2,1)S(1)}, u32[]{:S(2)}, u32[]{:S(2)}) %all-to-all-start) | async-done | bytes 829472 | tf_op jit(solution)/shard_map/all_to_all | solution.py:314
  30.6 5.2 %pair_gradient.1 = bf16[8,2,72,360]{3,2,1,0:T(8,128)(2,1)} custom-call(s32[1]{0:T(128)} %bitcast.me_ref, f32[2]{0:T(128)S(1)} %add_cosine_fusion.area_ref, bf16[8,2,72,360]{3,2,1,0:T(8,128)(2,1)S(1)} %all-to-all-done.f_ref, bf16[72,360]{1,0:T(8,128)(2,1)S(1)} %constant_dynamic-slice_fusion.t_ref), custom_call_target="tpu_custom_call" | custom-call | tf_op jit(solution)/shard_map/pair_gradient/pallas_call | solution.py:171
  35.8 3.9 %all-to-all-start.1 = ((bf16[8,2,72,360]{3,2,1,0:T(8,128)(2,1)}), bf16[8,2,72,360]{3,2,1,0:T(8,128)(2,1)S(1)}, u32[]{:S(2)}, u32[]{:S(2)}) async-start(bf16[8,2,72,360]{3,2,1,0:T(8,128)(2,1)} %pair_gradient.1), calls=%async_computation.1 | async-start | bytes 1769472 | tf_op jit(solution)/shard_map/all_to_all | solution.py:319
  39.7 10.3 %decoder_gates_1.1 = (bf16[2,2880,1024]{2,1,0:T(8,128)(2,1)}, f32[2,2880,1024]{2,1,0:T(8,128)}) custom-call(bf16[2,2880,256]{2,1,0:T(8,128)(2,1)} %bitcast.19, bf16[1024,256]{1,0:T(8,128)(2,1)} %w_in_ref.7, f32[1,1024]{1,0:T(1,128)} %bitcast.25, bf16[2,2880,1024]{2,1,0:T(8,128)(2,1)} %get-tuple-element.21.refs_0_, ...), custom_call_target="tpu_custom_call", output_to_operand_aliasing={{0}: (3, {}), {1}: (4, {})} | custom-call | flops 8000000000 | bytes 20000000 | tf_op jit(solution)/shard_map/decoder_gates_1/pallas_call | solution.py:117
  50.0 2.0 %all-to-all-done.1.d_ref = bf16[8,2,72,360]{3,2,1,0:T(8,128)(2,1)S(1)} async-done(((bf16[8,2,72,360]{3,2,1,0:T(8,128)(2,1)}), bf16[8,2,72,360]{3,2,1,0:T(8,128)(2,1)S(1)}, u32[]{:S(2)}, u32[]{:S(2)}) %all-to-all-start.1) | async-done | bytes 829472 | tf_op jit(solution)/shard_map/all_to_all | solution.py:319
  52.1 0.0 copy-start.1
  52.1 0.9 copy-done.1
  53.0 18.9 %decoder_backward.1 = (bf16[2,2880,256]{2,1,0:T(8,128)(2,1)}, f32[2,1344,128]{2,1,0:T(8,128)}) custom-call(bf16[8,2,72,360]{3,2,1,0:T(8,128)(2,1)} %copy-done.1, bf16[2,2880,1024]{2,1,0:T(8,128)(2,1)} %get-tuple-element.23.act_ref, f32[2,2880,1024]{2,1,0:T(8,128)} %get-tuple-element.24.gp_ref, bf16[2,2880,256]{2,1,0:T(8,128)(2,1)} %bitcast.20, ...), custom_call_target="tpu_custom_call" | custom-call | tf_op jit(solution)/shard_map/decoder_backward/pallas_call | solution.py:224
  71.9 1.1 fusion.1
  73.0 2.6 %collective-permute-start = (bf16[1344,128]{1,0:T(8,128)(2,1)S(1)}, bf16[1344,128]{1,0:T(8,128)(2,1)S(1)}, u32[]{:S(2)}, u32[]{:S(2)}) collective-permute-start(bf16[1344,128]{1,0:T(8,128)(2,1)S(1)} %fusion.1), channel_id=1, source_target_pairs={{0,1},{1,0},{2,3},{3,2},{4,5},{5,4},{6,7},{7,6},{8,9},{9,8},{10,11... | collective-permute-start | bytes 1032200 | tf_op jit(solution)/shard_map/ppermute | solution.py:286
  75.7 1.3 collective-permute-done
  76.9 1.2 fusion
  78.2 12.1 %all_to_all.25 = bf16[16,88,128]{2,1,0:T(8,128)(2,1)S(1)} all-to-all(bf16[16,88,128]{2,1,0:T(8,128)(2,1)S(1)} %bitcast.21), channel_id=1, replica_groups=mesh['y'=4,'xl'=2,'z'=8,'xh'=2,'c'=2] {'y','xl','xh'}, dimensions={0} | all-to-all | bytes 720896 | tf_op jit(solution)/shard_map/all_to_all | solution.py:288
  90.2 0.1 convert_reduce_fusion
  90.3 19.2 %all_to_all.26 = f32[8,88,128]{2,1,0:T(8,128)S(1)} all-to-all(f32[8,88,128]{2,1,0:T(8,128)S(1)} %broadcast_in_dim.20), channel_id=1, replica_groups=mesh['y'=4,'xl'=2,'z'=8,'xh'=2,'c'=2] {'z'}, dimensions={0} | all-to-all | bytes 720896 | tf_op jit(solution)/shard_map/all_to_all | solution.py:290
  109.6 12.6 %all_to_all.27 = bf16[16,88,128]{2,1,0:T(8,128)(2,1)S(1)} all-to-all(bf16[16,88,128]{2,1,0:T(8,128)(2,1)S(1)} %broadcast_in_dim.21), channel_id=1, replica_groups=mesh['y'=4,'xl'=2,'z'=8,'xh'=2,'c'=2] {'y','xl','xh'}, dimensions={0} | all-to-all | bytes 720896 | tf_op jit(solution)/shard_map/all_to_all | solution.py:294
  122.2 4.2 %collective-permute-start.1 = (bf16[1344,128]{1,0:T(8,128)(2,1)S(1)}, bf16[1344,128]{1,0:T(8,128)(2,1)S(1)}, u32[]{:S(2)}, u32[]{:S(2)}) collective-permute-start(bf16[1344,128]{1,0:T(8,128)(2,1)S(1)} %slice.4.mine_ref), channel_id=1, source_target_pairs={{0,1},{1,0},{2,3},{3,2},{4,5},{5,4},{6,7},{7,6},{8,9},{9,8},{10,11... | collective-permute-start | bytes 1032200 | tf_op jit(solution)/shard_map/ppermute | solution.py:297
  126.4 1.3 collective-permute-done.1.other_ref
  127.7 1.3 unpack_gradients.1
  (7 shorter events, 0.2 us)
Async XLA Ops:
  0.6 17.9 %copy-start = (bf16[72,2880]{1,0:T(8,128)(2,1)S(1)}, bf16[72,2880]{1,0:T(8,128)(2,1)}, u32[]{:S(2)}) copy-start(bf16[72,2880]{1,0:T(8,128)(2,1)} %param.12) | copy-start | bytes 1244164
  11.9 18.7 %all-to-all-start = ((bf16[8,2,72,360]{3,2,1,0:T(8,128)(2,1)}), bf16[8,2,72,360]{3,2,1,0:T(8,128)(2,1)S(1)}, u32[]{:S(2)}, u32[]{:S(2)}) async-start(bf16[8,2,72,360]{3,2,1,0:T(8,128)(2,1)} %decoder_forward.1), calls=%async_computation | async-start | bytes 1769472 | tf_op jit(solution)/shard_map/all_to_all | solution.py:314
  35.8 16.3 %all-to-all-start.1 = ((bf16[8,2,72,360]{3,2,1,0:T(8,128)(2,1)}), bf16[8,2,72,360]{3,2,1,0:T(8,128)(2,1)S(1)}, u32[]{:S(2)}, u32[]{:S(2)}) async-start(bf16[8,2,72,360]{3,2,1,0:T(8,128)(2,1)} %pair_gradient.1), calls=%async_computation.1 | async-start | bytes 1769472 | tf_op jit(solution)/shard_map/all_to_all | solution.py:319
  52.1 0.9 copy-start.1
  73.0 3.9 %collective-permute-start = (bf16[1344,128]{1,0:T(8,128)(2,1)S(1)}, bf16[1344,128]{1,0:T(8,128)(2,1)S(1)}, u32[]{:S(2)}, u32[]{:S(2)}) collective-permute-start(bf16[1344,128]{1,0:T(8,128)(2,1)S(1)} %fusion.1), channel_id=1, source_target_pairs={{0,1},{1,0},{2,3},{3,2},{4,5},{5,4},{6,7},{7,6},{8,9},{9,8},{10,11... | collective-permute-start | bytes 1032200 | tf_op jit(solution)/shard_map/ppermute | solution.py:286
  122.2 5.5 %collective-permute-start.1 = (bf16[1344,128]{1,0:T(8,128)(2,1)S(1)}, bf16[1344,128]{1,0:T(8,128)(2,1)S(1)}, u32[]{:S(2)}, u32[]{:S(2)}) collective-permute-start(bf16[1344,128]{1,0:T(8,128)(2,1)S(1)} %slice.4.mine_ref), channel_id=1, source_target_pairs={{0,1},{1,0},{2,3},{3,2},{4,5},{5,4},{6,7},{7,6},{8,9},{9,8},{10,11... | collective-permute-start | bytes 1032200 | tf_op jit(solution)/shard_map/ppermute | solution.py:297

commit v3 on v2

--- a/solution.py
+++ b/solution.py
@@ -178,16 +178,19 @@
     )(me, area, on_chip(block), goal)
 
 
-def bwd_kernel(d_ref, act_ref, gp_ref, hc_ref, w_out_ref, w_in_ref, cs_ref, g_ref, dpre_ref):
+def bwd_kernel(core_ref, d_ref, act_ref, gp_ref, hc_ref, w_out_ref, w_in_ref, cs_ref, keep_ref, give_ref, g_ref, dpre_ref):
     hid, latent = w_in_ref.shape
     chan = w_out_ref.shape[0]
-    first = (pl.program_id(0) == 0) & (pl.program_id(1) == 0)
+    per = hc_ref.shape[1] // PER
+    m, j = pl.program_id(0), pl.program_id(1)
+    first = (m == 0) & (j == 0)
+    last = (m == pl.num_programs(0) - 1) & (j == pl.num_programs(1) - 1)
 
     @pl.when(first)
     def _():
         g_ref[...] = jnp.zeros_like(g_ref)
 
-    d = jnp.concatenate([d_ref[i, 0] for i in range(d_ref.shape[0])], axis=1)
+    d = jnp.concatenate([d_ref[j * per + i, m] for i in range(per)], axis=1)
     d_t = d.astype(F32).T.astype(BF16)
     hc_t = hc_ref[0].astype(F32).T.astype(BF16)
     left = jnp.concatenate([hc_t, jnp.ones((16, hc_t.shape[1]), BF16)], axis=0)
@@ -215,17 +218,25 @@
     cs = jnp.dot(dpre_ref[...], w_in_ref[...], preferred_element_type=F32)
     cs_ref[0] = cs.astype(BF16)
 
-
-def decoder_backward(dfor, act, gp, codes, w_out, w_in):
+    @pl.when(last)
+    def _():
+        core = core_ref[0]
+        keep_ref[...] = g_ref[core]
+        give_ref[...] = g_ref[1 - core].astype(BF16)
+
+
+def decoder_backward(core, dfor, act, gp, codes, w_out, w_in):
     members, cells, latent = codes.shape
     hid = act.shape[2]
     chan = dfor.shape[2]
     rows = hid // 2 * (latent + 8 + chan) // 128
+    rows = -(-rows // (8 * lax.axis_size(PLANE))) * 8 * lax.axis_size(PLANE)
     return pl.pallas_call(
         bwd_kernel,
         grid=(members, cells // BBLK),
         in_specs=[
-            pl.BlockSpec((BBLK // PER, 1, chan, PER), lambda m, j: (j, m, 0, 0)),
+            SMEM,
+            VMEM,
             pl.BlockSpec((1, BBLK, hid), lambda m, j: (m, j, 0)),
             pl.BlockSpec((1, BBLK, hid), lambda m, j: (m, j, 0)),
             pl.BlockSpec((1, BBLK, latent), lambda m, j: (m, j, 0)),
@@ -234,16 +245,20 @@
         ],
         out_specs=[
             pl.BlockSpec((1, BBLK, latent), lambda m, j: (m, j, 0)),
-            whole((2, rows, 128)),
+            VMEM,
+            VMEM,
         ],
         out_shape=[
             jax.ShapeDtypeStruct((members, cells, latent), BF16),
-            jax.ShapeDtypeStruct((2, rows, 128), F32),
-        ],
-        scratch_shapes=[pltpu.VMEM((BBLK, hid), BF16)],
-        compiler_params=pltpu.CompilerParams(dimension_semantics=("arbitrary", "arbitrary")),
+            pltpu.VMEM((rows, 128), F32),
+            pltpu.VMEM((rows, 128), BF16),
+        ],
+        scratch_shapes=[pltpu.VMEM((2, rows, 128), F32), pltpu.VMEM((BBLK, hid), BF16)],
+        compiler_params=pltpu.CompilerParams(
+            dimension_semantics=("arbitrary", "arbitrary"), vmem_limit_bytes=48 * 2**20
+        ),
         name="decoder_backward",
-    )(dfor, act, gp, codes, w_out, w_in)
+    )(core, on_chip(dfor), act, gp, codes, *(pltpu.with_memory_space_constraint(w, pltpu.HBM) for w in (w_out, w_in)))
 
 
 def unpack_kernel(core_ref, mine_ref, other_ref, gi_ref, go_ref, gb_ref):
@@ -271,29 +286,25 @@
             jax.ShapeDtypeStruct((chan, hid), F32),
             jax.ShapeDtypeStruct((1, hid), F32),
         ],
+        compiler_params=limit(8),
         name="unpack_gradients",
     )(core, on_chip(mine), on_chip(other))
 
 
-def total_gradient(grads, scale):
-    _, rows, lanes = grads.shape
+def total_gradient(keep, give, scale):
+    rows, lanes = keep.shape
     plane = lax.axis_size(PLANE)
-    per = -(-rows // (8 * plane)) * 8
-    core = lax.axis_index("c")
     swap = [(0, 1), (1, 0)]
-    keep = lax.dynamic_index_in_dim(grads, core, 0, keepdims=False)
-    give = lax.dynamic_index_in_dim(grads, 1 - core, 0, keepdims=False).astype(BF16)
     both = (keep + lax.ppermute(give, "c", swap).astype(F32)).astype(BF16)
-    both = jnp.pad(both, ((0, plane * per - rows), (0, 0))).reshape(plane, per, lanes)
-    shares = lax.all_to_all(both, PLANE, 0, 0, tiled=True)
-    share = jnp.sum(shares.astype(F32), axis=0)
+    shares = lax.all_to_all(both.reshape(plane, rows // plane, lanes), PLANE, 0, 0, tiled=True)
+    share = (jnp.sum(shares.astype(F32), axis=0) * 0.5).astype(BF16)
     parts = lax.all_to_all(
         jnp.broadcast_to(share[None], (lax.axis_size("z"), *share.shape)), "z", 0, 0, tiled=True
     )
-    share = (jnp.sum(parts, axis=0) * scale).astype(BF16)
+    share = (jnp.sum(parts.astype(F32), axis=0) * (2.0 * scale)).astype(BF16)
     mine = lax.all_to_all(
         jnp.broadcast_to(share[None], (plane, *share.shape)), PLANE, 0, 0, tiled=True
-    ).reshape(plane * per, lanes)[:rows]
+    ).reshape(rows, lanes)
     return mine, lax.ppermute(mine, "c", swap)
 
 
@@ -319,9 +330,9 @@
     dfor_in = lax.all_to_all(dfor, MEMBER, 0, 0, tiled=True)
     later_b, _ = lax.optimization_barrier((b_row, dfor))
     act, gp = decoder_gates(1, codes, w_in, later_b, gates)
-    sensitivity, grads = decoder_backward(dfor_in, act, gp, codes, w_out, w_in)
-    mine, other = total_gradient(grads, 1.0 / math.sqrt(members * cells))
     core = lax.axis_index("c").astype(jnp.int32).reshape(1)
+    sensitivity, keep, give = decoder_backward(core, dfor_in, act, gp, codes, w_out, w_in)
+    mine, other = total_gradient(keep, give, 1.0 / math.sqrt(members * cells))
     grad_in, grad_out, grad_b = unpack(core, mine, other, hid, latent, chan)
     return jnp.swapaxes(sensitivity, 1, 2), grad_in, grad_out, grad_b[0]
 

time: 129 us -> 123 us (0.953)
  blocking collectives: 43.9 us -> 40.1 us
  local copies, waits for them, and re-layouts: 2.27 us -> 0.18 us
    all_to_all x1, blocking collectives: 19.2 us -> 16.5 us  [total_gradient(): lax.all_to_all(jnp.broadcast_to(share[None], (lax.axis_size('z'), *share....]
  transfers between devices with their start and end apart: 4 -> 4, of which waited for: 4 -> 4; matrix products, arithmetic and copies ran while one was open for 0% -> 0% of each run, Pallas kernels for 16% -> 17%
where the time goes in v3:
time: 123 us; the launch traced here: 122 us
  Pallas kernels  57.2 us (47%)
  blocking collectives  40.1 us (33%)
  starting transfers between devices  17.6 us (14%)
  waiting for transfers between devices  5.68 us (5%)
  between operations  1.36 us (1%)
    pallas_call x2, Pallas kernels, decoder_gates(): pl.pallas_call(gate_kernel, grid=(cells // BLK,), in_specs=[pl.BlockSpec(...  20.9 us
    pallas_call x1, Pallas kernels, decoder_backward(): pl.pallas_call(bwd_kernel, grid=(members, cells // BBLK), in_specs=[SMEM,...  18.7 us
    all_to_all x1, blocking collectives, total_gradient(): lax.all_to_all(jnp.broadcast_to(share[None], (lax.axis_size('z'), *share....  16.5 us
    all_to_all x1, blocking collectives, total_gradient(): lax.all_to_all(both.reshape(plane, rows // plane, lanes), PLANE, 0, 0, ti...  12.2 us
    all_to_all x1, blocking collectives, total_gradient(): lax.all_to_all(jnp.broadcast_to(share[None], (plane, *share.shape)), PLAN...  11.4 us
    pallas_call x1, Pallas kernels, decoder_forward(): pl.pallas_call(fwd_kernel, grid=(members,), in_specs=[pl.BlockSpec((1, ce...  11.2 us
    all_to_all x1, starting transfers between devices, on_device(): block = lax.all_to_all(forecast, MEMBER, 0, 0, tiled=True)  5.93 us
    pallas_call x1, Pallas kernels, pair_gradient(): pl.pallas_call(pair_kernel, in_specs=[SMEM, SMEM, VMEM, VMEM], out_specs=...  5.17 us
  transfers between devices with their start and end apart: 4, of which 4 were waited for; matrix products, arithmetic and copies ran while one was open for 0% of the time, Pallas kernels for 17%

profile of v3, /device:TPU:1, one launch (start us, length us, event | category | flops | bytes accessed | tf_op | source)
XLA Modules:
  0.0 122.3 jit_solution(17780160757911734290)
XLA Ops:
  0.6 0.0 copy-start
  0.6 11.2 %decoder_forward.1 = bf16[8,2,72,360]{3,2,1,0:T(8,128)(2,1)} custom-call(bf16[2,2880,256]{2,1,0:T(8,128)(2,1)} %bitcast.11, bf16[1024,256]{1,0:T(8,128)(2,1)} %w_in_ref.7, f32[1,1024]{1,0:T(1,128)} %bitcast.18, bf16[72,1024]{1,0:T(8,128)(2,1)} %w_out_ref.3, f32[1,72]{1,0:T(1,128)} %bitcast.21), custom_call_target="tpu_custom_call" | custom-call | tf_op jit(solution)/shard_map/decoder_forward/pallas_call | solution.py:80
  11.9 5.9 %all-to-all-start = ((bf16[8,2,72,360]{3,2,1,0:T(8,128)(2,1)}), bf16[8,2,72,360]{3,2,1,0:T(8,128)(2,1)S(1)}, u32[]{:S(2)}, u32[]{:S(2)}) async-start(bf16[8,2,72,360]{3,2,1,0:T(8,128)(2,1)} %decoder_forward.1), calls=%async_computation | async-start | bytes 1769472 | tf_op jit(solution)/shard_map/all_to_all | solution.py:325
  18.5 0.0 copy-done
  18.5 0.1 constant_dynamic-slice_fusion.t_ref
  18.6 10.4 %decoder_gates_0.1 = (bf16[2,2880,1024]{2,1,0:T(8,128)(2,1)}, f32[2,2880,1024]{2,1,0:T(8,128)}) custom-call(bf16[2,2880,256]{2,1,0:T(8,128)(2,1)} %bitcast.12, bf16[1024,256]{1,0:T(8,128)(2,1)} %w_in_ref.7, f32[1,1024]{1,0:T(1,128)} %bitcast.19), custom_call_target="tpu_custom_call" | custom-call | flops 8000000000 | bytes 20000000 | tf_op jit(solution)/shard_map/decoder_gates_0/pallas_call | solution.py:117
  29.0 1.6 %all-to-all-done.f_ref = bf16[8,2,72,360]{3,2,1,0:T(8,128)(2,1)S(1)} async-done(((bf16[8,2,72,360]{3,2,1,0:T(8,128)(2,1)}), bf16[8,2,72,360]{3,2,1,0:T(8,128)(2,1)S(1)}, u32[]{:S(2)}, u32[]{:S(2)}) %all-to-all-start) | async-done | bytes 829472 | tf_op jit(solution)/shard_map/all_to_all | solution.py:325
  30.6 5.2 %pair_gradient.1 = bf16[8,2,72,360]{3,2,1,0:T(8,128)(2,1)} custom-call(s32[1]{0:T(128)} %bitcast.1.me_ref, f32[2]{0:T(128)S(1)} %add_cosine_fusion.area_ref, bf16[8,2,72,360]{3,2,1,0:T(8,128)(2,1)S(1)} %all-to-all-done.f_ref, bf16[72,360]{1,0:T(8,128)(2,1)S(1)} %constant_dynamic-slice_fusion.t_ref), custom_call_target="tpu_custom_call" | custom-call | tf_op jit(solution)/shard_map/pair_gradient/pallas_call | solution.py:171
  35.8 4.2 %all-to-all-start.1 = ((bf16[8,2,72,360]{3,2,1,0:T(8,128)(2,1)}), bf16[8,2,72,360]{3,2,1,0:T(8,128)(2,1)}, u32[]{:S(2)}, u32[]{:S(2)}) async-start(bf16[8,2,72,360]{3,2,1,0:T(8,128)(2,1)} %pair_gradient.1), calls=%async_computation.1 | async-start | bytes 1769472 | tf_op jit(solution)/shard_map/all_to_all | solution.py:330
  40.0 0.0 copy-start.1
  40.0 10.5 %decoder_gates_1.1 = (bf16[2,2880,1024]{2,1,0:T(8,128)(2,1)}, f32[2,2880,1024]{2,1,0:T(8,128)}) custom-call(bf16[2,2880,256]{2,1,0:T(8,128)(2,1)} %bitcast.13, bf16[1024,256]{1,0:T(8,128)(2,1)} %w_in_ref.7, f32[1,1024]{1,0:T(1,128)} %bitcast.20, bf16[2,2880,1024]{2,1,0:T(8,128)(2,1)} %get-tuple-element.22.refs_0_, ...), custom_call_target="tpu_custom_call", output_to_operand_aliasing={{0}: (3, {}), {1}: (4, {})} | custom-call | flops 8000000000 | bytes 20000000 | tf_op jit(solution)/shard_map/decoder_gates_1/pallas_call | solution.py:117
  50.5 1.5 %all-to-all-done.1.d_ref = bf16[8,2,72,360]{3,2,1,0:T(8,128)(2,1)} async-done(((bf16[8,2,72,360]{3,2,1,0:T(8,128)(2,1)}), bf16[8,2,72,360]{3,2,1,0:T(8,128)(2,1)}, u32[]{:S(2)}, u32[]{:S(2)}) %all-to-all-start.1) | async-done | bytes 829472 | tf_op jit(solution)/shard_map/all_to_all | solution.py:330
  52.0 0.0 copy-done.1
  52.0 18.7 %decoder_backward.1 = (bf16[2,2880,256]{2,1,0:T(8,128)(2,1)}, f32[1408,128]{1,0:T(8,128)S(1)}, bf16[1408,128]{1,0:T(8,128)(2,1)S(1)}) custom-call(s32[1]{0:T(128)} %bitcast.core_ref, bf16[8,2,72,360]{3,2,1,0:T(8,128)(2,1)} %all-to-all-done.1.d_ref, bf16[2,2880,1024]{2,1,0:T(8,128)(2,1)} %get-tuple-element.24.act_ref, ...), custom_call_target="tpu_custom_call" | custom-call | tf_op jit(solution)/shard_map/decoder_backward/pallas_call | solution.py:234
  70.7 3.0 %collective-permute-start = (bf16[1408,128]{1,0:T(8,128)(2,1)S(1)}, bf16[1408,128]{1,0:T(8,128)(2,1)S(1)}, u32[]{:S(2)}, u32[]{:S(2)}) collective-permute-start(bf16[1408,128]{1,0:T(8,128)(2,1)S(1)} %get-tuple-element.28), channel_id=1, source_target_pairs={{0,1},{1,0},{2,3},{3,2},{4,5},{5,4},{6,7},{7,6},{8,9},{9,8},{10,11... | collective-permute-start | bytes 1081352 | tf_op jit(solution)/shard_map/ppermute | solution.py:298
  73.6 1.3 %collective-permute-done = bf16[1408,128]{1,0:T(8,128)(2,1)S(1)} collective-permute-done((bf16[1408,128]{1,0:T(8,128)(2,1)S(1)}, bf16[1408,128]{1,0:T(8,128)(2,1)S(1)}, u32[]{:S(2)}, u32[]{:S(2)}) %collective-permute-start) | collective-permute-done | bytes 360480 | tf_op jit(solution)/shard_map/ppermute | solution.py:298
  74.9 0.1 add_convert_fusion
  75.0 12.2 %all_to_all.25 = bf16[16,88,128]{2,1,0:T(8,128)(2,1)S(1)} all-to-all(bf16[16,88,128]{2,1,0:T(8,128)(2,1)S(1)} %bitcast.17), channel_id=1, replica_groups=mesh['y'=4,'xl'=2,'z'=8,'xh'=2,'c'=2] {'y','xl','xh'}, dimensions={0} | all-to-all | bytes 720896 | tf_op jit(solution)/shard_map/all_to_all | solution.py:299
  87.2 0.1 convert_reduce_fusion
  87.3 16.5 %all_to_all.26 = bf16[8,88,128]{2,1,0:T(8,128)(2,1)S(1)} all-to-all(bf16[8,88,128]{2,1,0:T(8,128)(2,1)S(1)} %broadcast_in_dim.20), channel_id=1, replica_groups=mesh['y'=4,'xl'=2,'z'=8,'xh'=2,'c'=2] {'z'}, dimensions={0} | all-to-all | bytes 360448 | tf_op jit(solution)/shard_map/all_to_all | solution.py:301
  103.9 11.4 %all_to_all.27 = bf16[16,88,128]{2,1,0:T(8,128)(2,1)S(1)} all-to-all(bf16[16,88,128]{2,1,0:T(8,128)(2,1)S(1)} %broadcast_in_dim.21), channel_id=1, replica_groups=mesh['y'=4,'xl'=2,'z'=8,'xh'=2,'c'=2] {'y','xl','xh'}, dimensions={0} | all-to-all | bytes 720896 | tf_op jit(solution)/shard_map/all_to_all | solution.py:305
  115.3 4.5 %collective-permute-start.1 = (bf16[1408,128]{1,0:T(8,128)(2,1)S(1)}, bf16[1408,128]{1,0:T(8,128)(2,1)S(1)}, u32[]{:S(2)}, u32[]{:S(2)}) collective-permute-start(bf16[1408,128]{1,0:T(8,128)(2,1)S(1)} %bitcast.15), channel_id=1, source_target_pairs={{0,1},{1,0},{2,3},{3,2},{4,5},{5,4},{6,7},{7,6},{8,9},{9,8},{10,11... | collective-permute-start | bytes 1081352 | tf_op jit(solution)/shard_map/ppermute | solution.py:308
  119.8 1.3 %collective-permute-done.1.other_ref = bf16[1408,128]{1,0:T(8,128)(2,1)S(1)} collective-permute-done((bf16[1408,128]{1,0:T(8,128)(2,1)S(1)}, bf16[1408,128]{1,0:T(8,128)(2,1)S(1)}, u32[]{:S(2)}, u32[]{:S(2)}) %collective-permute-start.1) | collective-permute-done | bytes 360480 | tf_op jit(solution)/shard_map/ppermute | solution.py:308
  121.1 1.3 %unpack_gradients.1 = (f32[1024,256]{1,0:T(8,128)}, f32[72,1024]{1,0:T(8,128)}, f32[1,1024]{1,0:T(1,128)}) custom-call(s32[1]{0:T(128)} %bitcast.core_ref, bf16[1408,128]{1,0:T(8,128)(2,1)S(1)} %bitcast.16, bf16[1408,128]{1,0:T(8,128)(2,1)S(1)} %collective-permute-done.1.other_ref), custom_call_target="tpu_custom_call" | custom-call | tf_op jit(solution)/shard_map/unpack_gradients/pallas_call | solution.py:280
  (6 shorter events, 0.2 us)
Async XLA Ops:
  0.6 17.9 %copy-start = (bf16[72,2880]{1,0:T(8,128)(2,1)S(1)}, bf16[72,2880]{1,0:T(8,128)(2,1)}, u32[]{:S(2)}) copy-start(bf16[72,2880]{1,0:T(8,128)(2,1)} %param.12) | copy-start | bytes 1244164
  11.9 18.7 %all-to-all-start = ((bf16[8,2,72,360]{3,2,1,0:T(8,128)(2,1)}), bf16[8,2,72,360]{3,2,1,0:T(8,128)(2,1)S(1)}, u32[]{:S(2)}, u32[]{:S(2)}) async-start(bf16[8,2,72,360]{3,2,1,0:T(8,128)(2,1)} %decoder_forward.1), calls=%async_computation | async-start | bytes 1769472 | tf_op jit(solution)/shard_map/all_to_all | solution.py:325
  35.8 16.2 %all-to-all-start.1 = ((bf16[8,2,72,360]{3,2,1,0:T(8,128)(2,1)}), bf16[8,2,72,360]{3,2,1,0:T(8,128)(2,1)}, u32[]{:S(2)}, u32[]{:S(2)}) async-start(bf16[8,2,72,360]{3,2,1,0:T(8,128)(2,1)} %pair_gradient.1), calls=%async_computation.1 | async-start | bytes 1769472 | tf_op jit(solution)/shard_map/all_to_all | solution.py:330
  40.0 12.0 %copy-start.1 = (bf16[2,256,2880]{1,2,0:T(8,128)(2,1)S(1)}, bf16[2,256,2880]{1,2,0:T(8,128)(2,1)}, u32[]{:S(2)}) copy-start(bf16[2,256,2880]{1,2,0:T(8,128)(2,1)} %param.7) | copy-start | bytes 8847364
  70.7 4.3 %collective-permute-start = (bf16[1408,128]{1,0:T(8,128)(2,1)S(1)}, bf16[1408,128]{1,0:T(8,128)(2,1)S(1)}, u32[]{:S(2)}, u32[]{:S(2)}) collective-permute-start(bf16[1408,128]{1,0:T(8,128)(2,1)S(1)} %get-tuple-element.28), channel_id=1, source_target_pairs={{0,1},{1,0},{2,3},{3,2},{4,5},{5,4},{6,7},{7,6},{8,9},{9,8},{10,11... | collective-permute-start | bytes 1081352 | tf_op jit(solution)/shard_map/ppermute | solution.py:298
  115.3 5.8 %collective-permute-start.1 = (bf16[1408,128]{1,0:T(8,128)(2,1)S(1)}, bf16[1408,128]{1,0:T(8,128)(2,1)S(1)}, u32[]{:S(2)}, u32[]{:S(2)}) collective-permute-start(bf16[1408,128]{1,0:T(8,128)(2,1)S(1)} %bitcast.15), channel_id=1, source_target_pairs={{0,1},{1,0},{2,3},{3,2},{4,5},{5,4},{6,7},{7,6},{8,9},{9,8},{10,11... | collective-permute-start | bytes 1081352 | tf_op jit(solution)/shard_map/ppermute | solution.py:308

commit v4 on v3

--- a/solution.py
+++ b/solution.py
@@ -13,7 +13,8 @@
 BLK = 2 * PER
 BBLK = 4 * PER
 SUB = 256
-FSUB = 512
+BSUB = 512
+FSUB = 1024
 C0 = math.sqrt(2.0 / math.pi)
 C1 = C0 * 0.044715
 F32 = jnp.float32
@@ -164,7 +165,7 @@
                 d_ref[m // local, m % local, rows, lanes] = d.astype(BF16)
         return carry
 
-    lax.fori_loop(0, chan // 8, strip, 0)
+    lax.fori_loop(0, chan // 8, strip, 0, unroll=3)
 
 
 def pair_gradient(me, area, block, goal):
@@ -198,19 +199,19 @@
     bias_end = latent + 8
 
     def slab(k):
-        cols = pl.ds(k * SUB, SUB)
-        dact = jnp.dot(d_t, half_out[:, k * SUB : (k + 1) * SUB], preferred_element_type=F32)
+        cols = pl.ds(k * BSUB, BSUB)
+        dact = jnp.dot(d_t, half_out[:, k * BSUB : (k + 1) * BSUB], preferred_element_type=F32)
         dpre_ref[:, cols] = (dact * gp_ref[0, :, cols]).astype(BF16)
 
     slab(0)
-    for k in range(hid // SUB):
-        if k + 1 < hid // SUB:
+    for k in range(hid // BSUB):
+        if k + 1 < hid // BSUB:
             slab(k + 1)
-        cols = pl.ds(k * SUB, SUB)
+        cols = pl.ds(k * BSUB, BSUB)
         g_in = jnp.dot(left, dpre_ref[:, cols], preferred_element_type=F32)
         g_out = jnp.dot(d, act_ref[0, :, cols], preferred_element_type=F32)
-        for i in range(SUB // 128):
-            c = k * (SUB // 128) + i
+        for i in range(BSUB // 128):
+            c = k * (BSUB // 128) + i
             half, base = c // 4, (c % 4) * (bias_end + chan)
             lanes = slice(i * 128, (i + 1) * 128)
             g_ref[half, base : base + bias_end, :] += g_in[:bias_end, lanes]

time: 123 us -> 122 us (level)
  no operation moved by 1% of the time
where the time goes in v4:
time: 122 us
  Pallas kernels  57 us (47%)
  blocking collectives  40 us (33%)
  starting transfers between devices  17.7 us (15%)
  waiting for transfers between devices  5.56 us (5%)
  between operations  1.36 us (1%)
    pallas_call x2, Pallas kernels, decoder_gates(): pl.pallas_call(gate_kernel, grid=(cells // BLK,), in_specs=[pl.BlockSpec(...  20.9 us
    pallas_call x1, Pallas kernels, decoder_backward(): pl.pallas_call(bwd_kernel, grid=(members, cells // BBLK), in_specs=[SMEM,...  18.7 us
    all_to_all x1, blocking collectives, total_gradient(): lax.all_to_all(jnp.broadcast_to(share[None], (lax.axis_size('z'), *share....  16.5 us
    all_to_all x1, blocking collectives, total_gradient(): lax.all_to_all(both.reshape(plane, rows // plane, lanes), PLANE, 0, 0, ti...  12.1 us
    all_to_all x1, blocking collectives, total_gradient(): lax.all_to_all(jnp.broadcast_to(share[None], (plane, *share.shape)), PLAN...  11.4 us
    pallas_call x1, Pallas kernels, decoder_forward(): pl.pallas_call(fwd_kernel, grid=(members,), in_specs=[pl.BlockSpec((1, ce...  11 us
    all_to_all x1, starting transfers between devices, on_device(): block = lax.all_to_all(forecast, MEMBER, 0, 0, tiled=True)  5.93 us
    pallas_call x1, Pallas kernels, pair_gradient(): pl.pallas_call(pair_kernel, in_specs=[SMEM, SMEM, VMEM, VMEM], out_specs=...  5.09 us
  transfers between devices with their start and end apart: 4, of which 4 were waited for; matrix products, arithmetic and copies ran while one was open for 0% of the time, Pallas kernels for 17%

profile of v4, /device:TPU:1, one launch (start us, length us, event | category | flops | bytes accessed | tf_op | source)
XLA Modules:
  0.0 122.1 jit_solution(11054437104634155235)
XLA Ops:
  0.6 0.0 copy-start
  0.6 11.0 %decoder_forward.1 = bf16[8,2,72,360]{3,2,1,0:T(8,128)(2,1)} custom-call(bf16[2,2880,256]{2,1,0:T(8,128)(2,1)} %bitcast.11, bf16[1024,256]{1,0:T(8,128)(2,1)} %w_in_ref.7, f32[1,1024]{1,0:T(1,128)} %bitcast.18, bf16[72,1024]{1,0:T(8,128)(2,1)} %w_out_ref.3, f32[1,72]{1,0:T(1,128)} %bitcast.21), custom_call_target="tpu_custom_call" | custom-call | tf_op jit(solution)/shard_map/decoder_forward/pallas_call | solution.py:81
  11.7 5.9 %all-to-all-start = ((bf16[8,2,72,360]{3,2,1,0:T(8,128)(2,1)}), bf16[8,2,72,360]{3,2,1,0:T(8,128)(2,1)S(1)}, u32[]{:S(2)}, u32[]{:S(2)}) async-start(bf16[8,2,72,360]{3,2,1,0:T(8,128)(2,1)} %decoder_forward.1), calls=%async_computation | async-start | bytes 1769472 | tf_op jit(solution)/shard_map/all_to_all | solution.py:326
  18.3 0.0 copy-done
  18.3 0.1 constant_dynamic-slice_fusion.t_ref
  18.4 10.4 %decoder_gates_0.1 = (bf16[2,2880,1024]{2,1,0:T(8,128)(2,1)}, f32[2,2880,1024]{2,1,0:T(8,128)}) custom-call(bf16[2,2880,256]{2,1,0:T(8,128)(2,1)} %bitcast.12, bf16[1024,256]{1,0:T(8,128)(2,1)} %w_in_ref.7, f32[1,1024]{1,0:T(1,128)} %bitcast.19), custom_call_target="tpu_custom_call" | custom-call | flops 8000000000 | bytes 20000000 | tf_op jit(solution)/shard_map/decoder_gates_0/pallas_call | solution.py:118
  28.8 1.6 %all-to-all-done.f_ref = bf16[8,2,72,360]{3,2,1,0:T(8,128)(2,1)S(1)} async-done(((bf16[8,2,72,360]{3,2,1,0:T(8,128)(2,1)}), bf16[8,2,72,360]{3,2,1,0:T(8,128)(2,1)S(1)}, u32[]{:S(2)}, u32[]{:S(2)}) %all-to-all-start) | async-done | bytes 829472 | tf_op jit(solution)/shard_map/all_to_all | solution.py:326
  30.4 5.1 %pair_gradient.1 = bf16[8,2,72,360]{3,2,1,0:T(8,128)(2,1)} custom-call(s32[1]{0:T(128)} %bitcast.1.me_ref, f32[2]{0:T(128)S(1)} %add_cosine_fusion.area_ref, bf16[8,2,72,360]{3,2,1,0:T(8,128)(2,1)S(1)} %all-to-all-done.f_ref, bf16[72,360]{1,0:T(8,128)(2,1)S(1)} %constant_dynamic-slice_fusion.t_ref), custom_call_target="tpu_custom_call" | custom-call | tf_op jit(solution)/shard_map/pair_gradient/pallas_call | solution.py:172
  35.5 4.4 %all-to-all-start.1 = ((bf16[8,2,72,360]{3,2,1,0:T(8,128)(2,1)}), bf16[8,2,72,360]{3,2,1,0:T(8,128)(2,1)}, u32[]{:S(2)}, u32[]{:S(2)}) async-start(bf16[8,2,72,360]{3,2,1,0:T(8,128)(2,1)} %pair_gradient.1), calls=%async_computation.1 | async-start | bytes 1769472 | tf_op jit(solution)/shard_map/all_to_all | solution.py:331
  39.9 0.0 copy-start.1
  39.9 10.5 %decoder_gates_1.1 = (bf16[2,2880,1024]{2,1,0:T(8,128)(2,1)}, f32[2,2880,1024]{2,1,0:T(8,128)}) custom-call(bf16[2,2880,256]{2,1,0:T(8,128)(2,1)} %bitcast.13, bf16[1024,256]{1,0:T(8,128)(2,1)} %w_in_ref.7, f32[1,1024]{1,0:T(1,128)} %bitcast.20, bf16[2,2880,1024]{2,1,0:T(8,128)(2,1)} %get-tuple-element.22.refs_0_, ...), custom_call_target="tpu_custom_call", output_to_operand_aliasing={{0}: (3, {}), {1}: (4, {})} | custom-call | flops 8000000000 | bytes 20000000 | tf_op jit(solution)/shard_map/decoder_gates_1/pallas_call | solution.py:118
  50.4 1.3 %all-to-all-done.1.d_ref = bf16[8,2,72,360]{3,2,1,0:T(8,128)(2,1)} async-done(((bf16[8,2,72,360]{3,2,1,0:T(8,128)(2,1)}), bf16[8,2,72,360]{3,2,1,0:T(8,128)(2,1)}, u32[]{:S(2)}, u32[]{:S(2)}) %all-to-all-start.1) | async-done | bytes 829472 | tf_op jit(solution)/shard_map/all_to_all | solution.py:331
  51.8 0.0 copy-done.1
  51.8 18.7 %decoder_backward.1 = (bf16[2,2880,256]{2,1,0:T(8,128)(2,1)}, f32[1408,128]{1,0:T(8,128)S(1)}, bf16[1408,128]{1,0:T(8,128)(2,1)S(1)}) custom-call(s32[1]{0:T(128)} %bitcast.core_ref, bf16[8,2,72,360]{3,2,1,0:T(8,128)(2,1)} %all-to-all-done.1.d_ref, bf16[2,2880,1024]{2,1,0:T(8,128)(2,1)} %get-tuple-element.24.act_ref, ...), custom_call_target="tpu_custom_call" | custom-call | tf_op jit(solution)/shard_map/decoder_backward/pallas_call | solution.py:235
  70.5 2.9 %collective-permute-start = (bf16[1408,128]{1,0:T(8,128)(2,1)S(1)}, bf16[1408,128]{1,0:T(8,128)(2,1)S(1)}, u32[]{:S(2)}, u32[]{:S(2)}) collective-permute-start(bf16[1408,128]{1,0:T(8,128)(2,1)S(1)} %get-tuple-element.28), channel_id=1, source_target_pairs={{0,1},{1,0},{2,3},{3,2},{4,5},{5,4},{6,7},{7,6},{8,9},{9,8},{10,11... | collective-permute-start | bytes 1081352 | tf_op jit(solution)/shard_map/ppermute | solution.py:299
  73.4 1.3 %collective-permute-done = bf16[1408,128]{1,0:T(8,128)(2,1)S(1)} collective-permute-done((bf16[1408,128]{1,0:T(8,128)(2,1)S(1)}, bf16[1408,128]{1,0:T(8,128)(2,1)S(1)}, u32[]{:S(2)}, u32[]{:S(2)}) %collective-permute-start) | collective-permute-done | bytes 360480 | tf_op jit(solution)/shard_map/ppermute | solution.py:299
  74.7 0.1 add_convert_fusion
  74.8 12.1 %all_to_all.25 = bf16[16,88,128]{2,1,0:T(8,128)(2,1)S(1)} all-to-all(bf16[16,88,128]{2,1,0:T(8,128)(2,1)S(1)} %bitcast.17), channel_id=1, replica_groups=mesh['y'=4,'xl'=2,'z'=8,'xh'=2,'c'=2] {'y','xl','xh'}, dimensions={0} | all-to-all | bytes 720896 | tf_op jit(solution)/shard_map/all_to_all | solution.py:300
  86.9 0.1 convert_reduce_fusion
  87.0 16.5 %all_to_all.26 = bf16[8,88,128]{2,1,0:T(8,128)(2,1)S(1)} all-to-all(bf16[8,88,128]{2,1,0:T(8,128)(2,1)S(1)} %broadcast_in_dim.20), channel_id=1, replica_groups=mesh['y'=4,'xl'=2,'z'=8,'xh'=2,'c'=2] {'z'}, dimensions={0} | all-to-all | bytes 360448 | tf_op jit(solution)/shard_map/all_to_all | solution.py:302
  103.6 11.4 %all_to_all.27 = bf16[16,88,128]{2,1,0:T(8,128)(2,1)S(1)} all-to-all(bf16[16,88,128]{2,1,0:T(8,128)(2,1)S(1)} %broadcast_in_dim.21), channel_id=1, replica_groups=mesh['y'=4,'xl'=2,'z'=8,'xh'=2,'c'=2] {'y','xl','xh'}, dimensions={0} | all-to-all | bytes 720896 | tf_op jit(solution)/shard_map/all_to_all | solution.py:306
  115.0 4.5 %collective-permute-start.1 = (bf16[1408,128]{1,0:T(8,128)(2,1)S(1)}, bf16[1408,128]{1,0:T(8,128)(2,1)S(1)}, u32[]{:S(2)}, u32[]{:S(2)}) collective-permute-start(bf16[1408,128]{1,0:T(8,128)(2,1)S(1)} %bitcast.15), channel_id=1, source_target_pairs={{0,1},{1,0},{2,3},{3,2},{4,5},{5,4},{6,7},{7,6},{8,9},{9,8},{10,11... | collective-permute-start | bytes 1081352 | tf_op jit(solution)/shard_map/ppermute | solution.py:309
  119.5 1.3 %collective-permute-done.1.other_ref = bf16[1408,128]{1,0:T(8,128)(2,1)S(1)} collective-permute-done((bf16[1408,128]{1,0:T(8,128)(2,1)S(1)}, bf16[1408,128]{1,0:T(8,128)(2,1)S(1)}, u32[]{:S(2)}, u32[]{:S(2)}) %collective-permute-start.1) | collective-permute-done | bytes 360480 | tf_op jit(solution)/shard_map/ppermute | solution.py:309
  120.8 1.3 %unpack_gradients.1 = (f32[1024,256]{1,0:T(8,128)}, f32[72,1024]{1,0:T(8,128)}, f32[1,1024]{1,0:T(1,128)}) custom-call(s32[1]{0:T(128)} %bitcast.core_ref, bf16[1408,128]{1,0:T(8,128)(2,1)S(1)} %bitcast.16, bf16[1408,128]{1,0:T(8,128)(2,1)S(1)} %collective-permute-done.1.other_ref), custom_call_target="tpu_custom_call" | custom-call | tf_op jit(solution)/shard_map/unpack_gradients/pallas_call | solution.py:281
  (6 shorter events, 0.2 us)
Async XLA Ops:
  0.6 17.7 %copy-start = (bf16[72,2880]{1,0:T(8,128)(2,1)S(1)}, bf16[72,2880]{1,0:T(8,128)(2,1)}, u32[]{:S(2)}) copy-start(bf16[72,2880]{1,0:T(8,128)(2,1)} %param.12) | copy-start | bytes 1244164
  11.7 18.7 %all-to-all-start = ((bf16[8,2,72,360]{3,2,1,0:T(8,128)(2,1)}), bf16[8,2,72,360]{3,2,1,0:T(8,128)(2,1)S(1)}, u32[]{:S(2)}, u32[]{:S(2)}) async-start(bf16[8,2,72,360]{3,2,1,0:T(8,128)(2,1)} %decoder_forward.1), calls=%async_computation | async-start | bytes 1769472 | tf_op jit(solution)/shard_map/all_to_all | solution.py:326
  35.5 16.3 %all-to-all-start.1 = ((bf16[8,2,72,360]{3,2,1,0:T(8,128)(2,1)}), bf16[8,2,72,360]{3,2,1,0:T(8,128)(2,1)}, u32[]{:S(2)}, u32[]{:S(2)}) async-start(bf16[8,2,72,360]{3,2,1,0:T(8,128)(2,1)} %pair_gradient.1), calls=%async_computation.1 | async-start | bytes 1769472 | tf_op jit(solution)/shard_map/all_to_all | solution.py:331
  39.9 11.9 %copy-start.1 = (bf16[2,256,2880]{1,2,0:T(8,128)(2,1)S(1)}, bf16[2,256,2880]{1,2,0:T(8,128)(2,1)}, u32[]{:S(2)}) copy-start(bf16[2,256,2880]{1,2,0:T(8,128)(2,1)} %param.7) | copy-start | bytes 8847364
  70.5 4.2 %collective-permute-start = (bf16[1408,128]{1,0:T(8,128)(2,1)S(1)}, bf16[1408,128]{1,0:T(8,128)(2,1)S(1)}, u32[]{:S(2)}, u32[]{:S(2)}) collective-permute-start(bf16[1408,128]{1,0:T(8,128)(2,1)S(1)} %get-tuple-element.28), channel_id=1, source_target_pairs={{0,1},{1,0},{2,3},{3,2},{4,5},{5,4},{6,7},{7,6},{8,9},{9,8},{10,11... | collective-permute-start | bytes 1081352 | tf_op jit(solution)/shard_map/ppermute | solution.py:299
  115.0 5.8 %collective-permute-start.1 = (bf16[1408,128]{1,0:T(8,128)(2,1)S(1)}, bf16[1408,128]{1,0:T(8,128)(2,1)S(1)}, u32[]{:S(2)}, u32[]{:S(2)}) collective-permute-start(bf16[1408,128]{1,0:T(8,128)(2,1)S(1)} %bitcast.15), channel_id=1, source_target_pairs={{0,1},{1,0},{2,3},{3,2},{4,5},{5,4},{6,7},{7,6},{8,9},{9,8},{10,11... | collective-permute-start | bytes 1081352 | tf_op jit(solution)/shard_map/ppermute | solution.py:309
